TPU v7x, 256 devices: a whole 4x4x8 slice. The times are simulated.
256 devices in a mesh: dp: 8 (over x, core), expert: 32 (over y, z).
Axes of the slice: x: 4, y: 4, z: 8, core: 2. Of those that a mesh axis runs over, the one named last changes fastest.
Arguments:
- queries: bfloat16 [2, 8, 32, 2048], P(None, 'dp', 'expert'), may hold values from -5 to 5
- cache_keys: bfloat16 [8, 32, 512, 512], P('dp', 'expert'), may hold values from -5 to 5
- cache_values: bfloat16 [8, 32, 512, 512], P('dp', 'expert'), may hold values from -6 to 6
- new_keys: bfloat16 [2, 8, 32, 512], P(None, 'dp', 'expert'), may hold values from -9 to 9
- new_values: bfloat16 [2, 8, 32, 512], P(None, 'dp', 'expert'), may hold values from -6 to 6
- cache_len: int32 [8, 32], P('dp', 'expert'), may hold values from 256 to 510, as said below
- o_proj: bfloat16 [2048, 4096], P(None, 'expert'), may hold values from -0.125 to 0.125
- residual_in: bfloat16 [2, 8, 32, 4096], P(None, 'dp', None, 'expert'), may hold values from -36 to 36
- norm_gain: float32 [4096], P('expert'), may hold values from 0.1 to 1.9
- router: float32 [4096, 8], P('expert'), may hold values from -0.09375 to 0.09375
- expert_gate: bfloat16 [32, 4096, 3584], P('expert', None, 'dp'), may hold values from -0.09375 to 0.09375
- expert_up: bfloat16 [32, 4096, 3584], P('expert', None, 'dp'), may hold values from -0.09375 to 0.09375
- expert_down: bfloat16 [32, 3584, 4096], P('expert', 'dp'), may hold values from -0.046875 to 0.046875
- routes: int32 [2, 8, 32, 2], replicated, may hold values from 0 to 7, all different within a row; in each aligned block of 32 rows (0 to 31, 32 to 63, ..., all dimensions but the last counted through in order) at most 16 rows name the same one
- answers: int32 [2, 8, 32], P(None, 'dp', 'expert'), may hold values from 0 to 127
- stop_mask: int32 [2, 8], P(None, 'dp'), may hold values 0 or 1
Outputs:
- residual_out: bfloat16 [2, 8, 32, 4096], P(None, 'dp', None, 'expert')
- vote_share: float32 [2, 8, 128], P(None, 'dp')
Inputs may be any that keep to these rules, and one draw needn't show every extreme that they name: `cache_len`: some sequence uses exactly 510 cached positions. `routes`: each token names 2 different experts; in each step, the tokens of the 1 prompts of one index of dp (all their samples together) name one expert at most 16 times.
All inputs are finite; a program needn't handle non-finite values. No bound on the sum of `stop_mask` on one device may be relied on, other than what follows from the above.
Results may differ from a plain program's by a relative error of at most 0.0055.
Values may be sent and summed in bfloat16 or wider, within the bound.
A program may use at most 64 MiB of HBM per device.

v0:
```python
import jax
import jax.numpy as jnp
from jax import lax
from jax.sharding import PartitionSpec as P

D = 4096
E = 8
TOP = 2
HD = 128
QH = 16
KVH = 4
STEPS = 2
ANSWERS = 128


EPSILON = 1e-05


def from_everyone(array, axis):
    copies = jnp.broadcast_to(array, (lax.axis_size(axis), *array.shape))
    return lax.all_to_all(copies, axis, split_axis=0, concat_axis=0, tiled=True)


def joined_along(blocks, dim):
    blocks = jnp.moveaxis(blocks, 0, dim)
    dims = blocks.shape
    return blocks.reshape(*dims[:dim], dims[dim] * dims[dim + 1], *dims[dim + 2 :])


def gathered_copies(array, axis, dim):
    blocks = from_everyone(array, axis)
    return joined_along(blocks, dim)


def cut_along(array, dim, devices):
    before, after = (array.shape[:dim], array.shape[dim + 1 :])
    return jnp.moveaxis(array.reshape(*before, devices, -1, *after), dim, 0)


def sent_and_summed(array, axis, dim):
    blocks = cut_along(array, dim, lax.axis_size(axis))
    arrived = lax.all_to_all(blocks, axis, split_axis=0, concat_axis=0, tiled=True)
    return arrived.astype(jnp.float32).sum(axis=0)


def of_everyone(array, axis):
    return from_everyone(array, axis).sum(axis=0)


def packed_total(arrays, axis):
    ends = [0]
    for a in arrays:
        ends.append(ends[-1] + a.size)
    so_far = of_everyone(jnp.concatenate([a.ravel() for a in arrays]), axis)
    return tuple((so_far[b:e].reshape(a.shape) for a, b, e in zip(arrays, ends, ends[1:])))


def attend(query, keys, values, fresh_keys, fresh_values, lengths):
    step_count = query.shape[0]
    row_count = query.shape[1]
    cache_size = keys.shape[1]
    group_size = QH // KVH
    score_scale = HD ** (-0.5)
    queried = query.reshape(step_count, row_count, KVH, group_size, HD)
    old_keys = keys.reshape(row_count, cache_size, KVH, HD)
    old_values = values.reshape(row_count, cache_size, KVH, HD)
    young_keys = fresh_keys.reshape(step_count, row_count, KVH, HD)
    young_values = fresh_values.reshape(step_count, row_count, KVH, HD)
    old_scores = (
        jnp.einsum("trkgd,rckd->rkgtc", queried, old_keys, preferred_element_type=jnp.float32)
        * score_scale
    )
    new_scores = (
        jnp.einsum("trkgd,urkd->rkgtu", queried, young_keys, preferred_element_type=jnp.float32)
        * score_scale
    )
    old_valid = jnp.arange(cache_size, dtype=jnp.int32)[None, :] < lengths[:, None]
    old_scores = jnp.where(old_valid[:, None, None, None, :], old_scores, -jnp.inf)
    new_valid = jnp.arange(step_count)[None, :] <= jnp.arange(step_count)[:, None]
    new_scores = jnp.where(new_valid, new_scores, -jnp.inf)
    highest = jnp.maximum(jnp.max(old_scores, -1), jnp.max(new_scores, -1))[..., None]
    old_exp = jnp.exp(old_scores - highest)
    new_exp = jnp.exp(new_scores - highest)
    denominator = jnp.sum(old_exp, -1, keepdims=True) + jnp.sum(new_exp, -1, keepdims=True)
    old_weights = (old_exp / denominator).astype(jnp.bfloat16)
    new_weights = (new_exp / denominator).astype(jnp.bfloat16)
    combined = jnp.einsum(
        "rkgtc,rckd->trkgd", old_weights, old_values, preferred_element_type=jnp.float32
    )
    combined = combined + jnp.einsum(
        "rkgtu,urkd->trkgd", new_weights, young_values, preferred_element_type=jnp.float32
    )
    return combined.reshape(step_count, row_count, QH * HD).astype(jnp.bfloat16)


def slot_tables(picks, capacity):
    block_count = picks.shape[0]
    row_count = picks.shape[1]
    expert_hot = (picks[..., None] == jnp.arange(E, dtype=jnp.int32)).astype(jnp.int32)
    expert_hot = expert_hot.reshape(block_count, row_count * TOP, E)
    earlier = jnp.cumsum(expert_hot, 1) - expert_hot
    place = jnp.sum(earlier * expert_hot, -1).reshape(block_count, row_count, TOP)
    slot_ids = picks * capacity + place
    return (slot_ids[..., None] == jnp.arange(E * capacity, dtype=jnp.int32)).astype(jnp.float32)


def on_device(
    queries,
    cache_keys,
    cache_values,
    new_keys,
    new_values,
    cache_len,
    o_proj,
    residual_in,
    norm_gain,
    router,
    expert_gate,
    expert_up,
    expert_down,
    routes,
    answers,
    stop_mask,
):
    prompt_dev = residual_in.shape[1]
    samples = residual_in.shape[2]
    columns = residual_in.shape[3]
    local_count = queries.shape[2]
    seq_count = prompt_dev * local_count
    cache_size = cache_keys.shape[2]
    spread = lax.axis_size("expert") // E
    capacity = 2 * prompt_dev * samples * TOP // E
    block_rows = prompt_dev * samples
    dp_index = lax.axis_index("dp")
    attended = attend(
        queries.reshape(STEPS, seq_count, QH * HD),
        cache_keys.reshape(seq_count, cache_size, KVH * HD),
        cache_values.reshape(seq_count, cache_size, KVH * HD),
        new_keys.reshape(STEPS, seq_count, KVH * HD),
        new_values.reshape(STEPS, seq_count, KVH * HD),
        cache_len.reshape(seq_count),
    ).reshape(STEPS, prompt_dev, local_count, QH * HD)
    active = (1 - stop_mask).astype(jnp.float32)
    attn_proj = jnp.einsum(
        "tpsq,qc->tpsc",
        gathered_copies(attended, "expert", 2),
        o_proj,
        preferred_element_type=jnp.float32,
    )
    mixed_rows = residual_in.astype(jnp.float32) + attn_proj
    squares = jnp.sum(mixed_rows * mixed_rows, -1)
    scaled = mixed_rows * norm_gain
    partial_logits = jnp.einsum("tpsc,ce->tpse", scaled, router, precision=lax.Precision.HIGHEST)
    squares_all, logit_sums = packed_total((squares, partial_logits), "expert")
    inv_rms = lax.rsqrt(squares_all / D + EPSILON)[..., None]
    logits = logit_sums * inv_rms
    normed_f = scaled * inv_rms
    normed = normed_f.astype(jnp.bfloat16)
    own_picks = lax.dynamic_slice_in_dim(routes, dp_index * prompt_dev, prompt_dev, 1)
    expert_hot = (own_picks[..., None] == jnp.arange(E, dtype=jnp.int32)).astype(jnp.float32)
    chosen = jnp.sum(expert_hot * logits[:, :, :, None, :], -1)
    gate_weights = jax.nn.sigmoid(chosen - chosen[..., ::-1]).reshape(STEPS, block_rows, TOP)
    own_table = slot_tables(own_picks.reshape(STEPS, block_rows, TOP), capacity)
    senders = jnp.sum(own_table, 2).astype(jnp.bfloat16)
    outgoing = jnp.einsum(
        "trs,trx->tsx",
        senders,
        normed.reshape(STEPS, block_rows, columns),
        preferred_element_type=jnp.float32,
    ).astype(jnp.bfloat16)
    outgoing = jnp.transpose(outgoing.reshape(STEPS, E, capacity, columns), (1, 0, 2, 3)).reshape(
        E, 1, STEPS * capacity, columns
    )
    outgoing = jnp.broadcast_to(outgoing, (E, spread, STEPS * capacity, columns)).reshape(
        E * spread, STEPS * capacity, columns
    )
    tokens = gathered_copies(
        lax.all_to_all(outgoing, "expert", split_axis=0, concat_axis=2, tiled=True), "dp", 0
    )
    gate_part = jnp.einsum(
        "...d,df->...f", tokens, expert_gate[0], preferred_element_type=jnp.float32
    )
    up_part = jnp.einsum("...d,df->...f", tokens, expert_up[0], preferred_element_type=jnp.float32)
    hidden = (jax.nn.silu(gate_part) * up_part).astype(jnp.bfloat16)
    partial_out = sent_and_summed(
        jnp.einsum(
            "...f,fd->...d", hidden, expert_down[0], preferred_element_type=jnp.float32
        ).astype(jnp.bfloat16),
        "dp",
        0,
    )
    returned = lax.all_to_all(
        partial_out.astype(jnp.bfloat16), "expert", split_axis=2, concat_axis=0, tiled=True
    ).astype(partial_out.dtype)
    slot_out = jnp.sum(returned.reshape(E, spread, STEPS, capacity, columns), 1)
    slot_out = jnp.transpose(slot_out, (1, 0, 2, 3)).reshape(STEPS, E * capacity, columns)
    combine = jnp.einsum("trk,trks->trs", gate_weights, own_table)
    moe = jnp.einsum("trs,tsx->trx", combine, slot_out, precision=lax.Precision.HIGHEST).reshape(
        STEPS, prompt_dev, samples, columns
    )
    updated = residual_in.astype(jnp.float32) + active[:, :, None, None] * (attn_proj + moe)
    hits = jnp.sum(
        (answers[..., None] == jnp.arange(ANSWERS, dtype=jnp.int32)).astype(jnp.float32), 2
    )
    votes = active[:, :, None] * hits
    tallied = of_everyone(votes, "expert")
    running = jnp.cumsum(tallied, 0)
    shares = running / jnp.maximum(jnp.sum(running, -1, keepdims=True), 1.0)
    return (updated.astype(jnp.bfloat16), shares)


def solution(mesh):
    placed = (
        P(None, "dp", "expert", None),
        P("dp", "expert", None, None),
        P("dp", "expert", None, None),
        P(None, "dp", "expert", None),
        P(None, "dp", "expert", None),
        P("dp", "expert"),
        P(None, "expert"),
        P(None, "dp", None, "expert"),
        P("expert"),
        P("expert", None),
        P("expert", None, "dp"),
        P("expert", None, "dp"),
        P("expert", "dp", None),
        P(),
        P(None, "dp", "expert"),
        P(None, "dp"),
    )
    return jax.shard_map(
        on_device,
        mesh=mesh,
        in_specs=placed,
        out_specs=(P(None, "dp", None, "expert"), P(None, "dp", None)),
        check_vma=False,
    )
```

profile of v0, /device:TPU:2, one launch (start us, length us, event | category | flops | bytes accessed | tf_op | source)
XLA Modules:
  0.0 197.3 jit_solution(6601510097964932942)
XLA Ops:
  1.5 1.2 reshape.308
  3.3 0.9 convolution_multiply_fusion.1
  5.0 1.2 reshape.312
  7.5 11.5 %all-to-all-start = ((bf16[32,2,1,1,2048]{4,1,3,2,0:T(2,128)(2,1)}), bf16[32,2,1,1,2048]{4,1,3,2,0:T(2,128)(2,1)S(1)}, u32[]{:S(2)}, u32[]{:S(2)}) async-start(bf16[32,2,1,1,2048]{4,1,3,2,0:T(2,128)(2,1)} %broadcast_in_dim.36), calls=%async_computation | async-start | bytes 524288 | tf_op jit(solution)/shard_map/all_to_all | solution.py:21
  20.4 11.0 %all-to-all-done = bf16[32,2,1,1,2048]{4,1,3,2,0:T(2,128)(2,1)S(1)} async-done(((bf16[32,2,1,1,2048]{4,1,3,2,0:T(2,128)(2,1)}), bf16[32,2,1,1,2048]{4,1,3,2,0:T(2,128)(2,1)S(1)}, u32[]{:S(2)}, u32[]{:S(2)}) %all-to-all-start) | async-done | bytes 262176 | tf_op jit(solution)/shard_map/all_to_all | solution.py:21
  32.8 4.4 %all-to-all-start.1 = ((f32[32,1,576]{2,1,0:T(1,128)}), f32[32,1,576]{2,1,0:T(1,128)S(1)}, u32[]{:S(2)}, u32[]{:S(2)}) async-start(f32[32,1,576]{2,1,0:T(1,128)} %broadcast_in_dim.37), calls=%async_computation.1 | async-start | bytes 163840 | tf_op jit(solution)/shard_map/all_to_all | solution.py:21
  38.0 9.4 %all-to-all-done.1 = f32[32,1,576]{2,1,0:T(1,128)S(1)} async-done(((f32[32,1,576]{2,1,0:T(1,128)}), f32[32,1,576]{2,1,0:T(1,128)S(1)}, u32[]{:S(2)}, u32[]{:S(2)}) %all-to-all-start.1) | async-done | bytes 73760 | tf_op jit(solution)/shard_map/all_to_all | solution.py:21
  47.9 14.2 %all_to_all.53 = bf16[32,32,128]{2,1,0:T(8,128)(2,1)S(1)} all-to-all(bf16[32,32,128]{2,1,0:T(8,128)(2,1)S(1)} %bitcast.193), channel_id=1, replica_groups=mesh['dp'=8,'expert'=32] {'expert'}, dimensions={0} | all-to-all | bytes 524288 | tf_op jit(solution)/shard_map/all_to_all | solution.py:178
  62.3 1.6 broadcast_in_dim.67
  63.9 4.8 %all-to-all-start.3 = ((bf16[8,1,32,4096]{3,2,1,0:T(8,128)(2,1)}), bf16[8,1,32,4096]{3,2,1,0:T(8,128)(2,1)S(1)}, u32[]{:S(2)}, u32[]{:S(2)}) async-start(bf16[8,1,32,4096]{3,2,1,0:T(8,128)(2,1)} %broadcast_in_dim.67), calls=%async_computation.3 | async-start | bytes 4194304 | tf_op jit(solution)/shard_map/all_to_all | solution.py:21
  68.8 25.6 %all-to-all-done.3 = bf16[8,1,32,4096]{3,2,1,0:T(8,128)(2,1)S(1)} async-done(((bf16[8,1,32,4096]{3,2,1,0:T(8,128)(2,1)}), bf16[8,1,32,4096]{3,2,1,0:T(8,128)(2,1)S(1)}, u32[]{:S(2)}, u32[]{:S(2)}) %all-to-all-start.3) | async-done | bytes 2097184 | tf_op jit(solution)/shard_map/all_to_all | solution.py:21
  95.0 4.5 %all-to-all-start.6 = ((f32[32,2,1,128]{3,2,1,0:T(1,128)}), f32[32,2,1,128]{3,2,1,0:T(1,128)S(1)}, u32[]{:S(2)}, u32[]{:S(2)}) async-start(f32[32,2,1,128]{3,2,1,0:T(1,128)} %broadcast_in_dim.68), calls=%async_computation.6 | async-start | bytes 65536 | tf_op jit(solution)/shard_map/all_to_all | solution.py:21
  99.5 3.3 %fusion.4 = f32[8,32,448]{2,1,0:T(8,128)S(1)} fusion(bf16[1,4096,448]{1,2,0:T(8,128)(2,1)} %param.26, bf16[8,1,32,4096]{3,2,1,0:T(8,128)(2,1)S(1)} %all-to-all-done.3), kind=kOutput, calls=%fused_computation.5 | convolution fusion | flops 939524096 | bytes 6225920 | tf_op jit(solution)/shard_map/...d,df->...f/dot_general | solution.py:180
  102.8 7.0 %fusion = bf16[8,1,32,4096]{3,2,1,0:T(8,128)(2,1)} fusion(bf16[1,448,4096]{2,1,0:T(8,128)(2,1)} %param.28, bf16[1,4096,448]{1,2,0:T(8,128)(2,1)} %param.27, bf16[8,1,32,4096]{3,2,1,0:T(8,128)(2,1)S(1)} %all-to-all-done.3, f32[8,32,448]{2,1,0:T(8,128)S(1)} %fusion.4), kind=kOutput, calls=%fused_computation.1 | convolution fusion | flops 1880784896 | bytes 11993088 | tf_op jit(solution)/shard_map/...f,fd->...d/dot_general | solution.py:186
  109.8 5.0 %all-to-all-start.4 = ((bf16[8,1,32,4096]{3,2,1,0:T(8,128)(2,1)}), bf16[8,1,32,4096]{3,2,1,0:T(8,128)(2,1)S(1)}, u32[]{:S(2)}, u32[]{:S(2)}) async-start(bf16[8,1,32,4096]{3,2,1,0:T(8,128)(2,1)} %fusion), calls=%async_computation.4 | async-start | bytes 4194304 | tf_op jit(solution)/shard_map/all_to_all | solution.py:42
  116.7 23.8 %all-to-all-done.4 = bf16[8,1,32,4096]{3,2,1,0:T(8,128)(2,1)S(1)} async-done(((bf16[8,1,32,4096]{3,2,1,0:T(8,128)(2,1)}), bf16[8,1,32,4096]{3,2,1,0:T(8,128)(2,1)S(1)}, u32[]{:S(2)}, u32[]{:S(2)}) %all-to-all-start.4) | async-done | bytes 2097184 | tf_op jit(solution)/shard_map/all_to_all | solution.py:42
  140.9 2.8 %copy.239 = bf16[1,32,4096]{1,0,2:T(2,128)(2,1)S(1)} copy(bf16[1,32,4096]{2,1,0:T(8,128)(2,1)S(1)} %bitcast.191) | data formatting | bytes 524288 | tf_op jit(solution)/shard_map/reduce_sum | solution.py:43
  144.2 23.4 %reduce.11 = bf16[4096,32]{1,0:T(8,128)(2,1)} reduce(bf16[4096,1,32]{2,1,0:T(2,128)(2,1)S(1)} %bitcast.188, bf16[]{:T(256)} %broadcast.158), dimensions={1}, to_apply=%bitcast.174.reduce_sub_computation | reduce | bytes 524290
  167.6 3.1 %reshape.340 = bf16[32,2,2048]{2,1,0:T(2,128)(2,1)} reshape(bf16[4096,32]{1,0:T(8,128)(2,1)} %reduce.11) | data formatting | bytes 524288
  170.6 9.8 %all-to-all-start.5 = ((bf16[32,2,2048]{2,1,0:T(2,128)(2,1)}), bf16[32,2,2048]{2,1,0:T(2,128)(2,1)S(1)}, u32[]{:S(2)}, u32[]{:S(2)}) async-start(bf16[32,2,2048]{2,1,0:T(2,128)(2,1)} %reshape.340), calls=%async_computation.5 | async-start | bytes 524288 | tf_op jit(solution)/shard_map/all_to_all | solution.py:192
  180.8 11.7 %all-to-all-done.5 = bf16[32,2,2048]{2,1,0:T(2,128)(2,1)S(1)} async-done(((bf16[32,2,2048]{2,1,0:T(2,128)(2,1)}), bf16[32,2,2048]{2,1,0:T(2,128)(2,1)S(1)}, u32[]{:S(2)}, u32[]{:S(2)}) %all-to-all-start.5) | async-done | bytes 262176 | tf_op jit(solution)/shard_map/all_to_all | solution.py:192
  192.5 1.4 reshape.341
  193.8 2.1 %copy.240 = bf16[1,32,4096]{2,1,0:T(8,128)(2,1)S(1)} copy(bf16[1,32,4096]{1,0,2:T(2,128)(2,1)S(1)} %bitcast.187) | data formatting | bytes 524288 | tf_op jit(solution)/shard_map/all_to_all | solution.py:192
  196.5 0.8 fusion.25
  (80 shorter events, 11.6 us)
Async XLA Ops:
  0.6 30.8 %copy-start = (bf16[2048,128]{1,0:T(8,128)(2,1)S(1)}, bf16[2048,128]{1,0:T(8,128)(2,1)}, u32[]{:S(2)}) copy-start(bf16[2048,128]{1,0:T(8,128)(2,1)} %param.22) | copy-start | bytes 1572868
  0.6 5.8 %copy-start.5 = (bf16[2,1,1,512]{3,0,2,1:T(2,128)(2,1)S(1)}, bf16[2,1,1,512]{3,0,2,1:T(2,128)(2,1)}, u32[]{:S(2)}) copy-start(bf16[2,1,1,512]{3,0,2,1:T(2,128)(2,1)} %param.20) | copy-start | bytes 6148
  0.7 30.8 %copy-start.1 = (bf16[2,1,32,128]{3,2,1,0:T(8,128)(2,1)S(1)}, bf16[2,1,32,128]{3,2,1,0:T(8,128)(2,1)}, u32[]{:S(2)}) copy-start(bf16[2,1,32,128]{3,2,1,0:T(8,128)(2,1)} %param.23) | copy-start | bytes 49156
  0.7 31.1 %copy-start.3 = (f32[128]{0:T(128)S(1)}, f32[128]{0:T(128)}, u32[]{:S(2)}) copy-start(f32[128]{0:T(128)} %param.24) | copy-start | bytes 1540
  0.7 31.1 %copy-start.2 = (f32[128,8]{0,1:T(8,128)S(1)}, f32[128,8]{0,1:T(8,128)}, u32[]{:S(2)}) copy-start(f32[128,8]{0,1:T(8,128)} %param.25) | copy-start | bytes 12292
  7.5 23.9 %all-to-all-start = ((bf16[32,2,1,1,2048]{4,1,3,2,0:T(2,128)(2,1)}), bf16[32,2,1,1,2048]{4,1,3,2,0:T(2,128)(2,1)S(1)}, u32[]{:S(2)}, u32[]{:S(2)}) async-start(bf16[32,2,1,1,2048]{4,1,3,2,0:T(2,128)(2,1)} %broadcast_in_dim.36), calls=%async_computation | async-start | bytes 524288 | tf_op jit(solution)/shard_map/all_to_all | solution.py:21
  32.8 14.6 %all-to-all-start.1 = ((f32[32,1,576]{2,1,0:T(1,128)}), f32[32,1,576]{2,1,0:T(1,128)S(1)}, u32[]{:S(2)}, u32[]{:S(2)}) async-start(f32[32,1,576]{2,1,0:T(1,128)} %broadcast_in_dim.37), calls=%async_computation.1 | async-start | bytes 163840 | tf_op jit(solution)/shard_map/all_to_all | solution.py:21
  62.1 6.6 %copy-start.6 = (s32[2,1]{0,1:T(1,128)S(1)}, s32[2,1]{0,1:T(1,128)}, u32[]{:S(2)}) copy-start(s32[2,1]{0,1:T(1,128)} %param.31) | copy-start | bytes 28
  62.2 6.6 %copy-start.4 = (s32[2,1,1]{0,2,1:T(1,128)S(1)}, s32[2,1,1]{0,2,1:T(1,128)}, u32[]{:S(2)}) copy-start(s32[2,1,1]{0,2,1:T(1,128)} %param.30) | copy-start | bytes 28
  63.9 30.5 %all-to-all-start.3 = ((bf16[8,1,32,4096]{3,2,1,0:T(8,128)(2,1)}), bf16[8,1,32,4096]{3,2,1,0:T(8,128)(2,1)S(1)}, u32[]{:S(2)}, u32[]{:S(2)}) async-start(bf16[8,1,32,4096]{3,2,1,0:T(8,128)(2,1)} %broadcast_in_dim.67), calls=%async_computation.3 | async-start | bytes 4194304 | tf_op jit(solution)/shard_map/all_to_all | solution.py:21
  95.0 14.8 %all-to-all-start.6 = ((f32[32,2,1,128]{3,2,1,0:T(1,128)}), f32[32,2,1,128]{3,2,1,0:T(1,128)S(1)}, u32[]{:S(2)}, u32[]{:S(2)}) async-start(f32[32,2,1,128]{3,2,1,0:T(1,128)} %broadcast_in_dim.68), calls=%async_computation.6 | async-start | bytes 65536 | tf_op jit(solution)/shard_map/all_to_all | solution.py:21
  109.8 30.7 %all-to-all-start.4 = ((bf16[8,1,32,4096]{3,2,1,0:T(8,128)(2,1)}), bf16[8,1,32,4096]{3,2,1,0:T(8,128)(2,1)S(1)}, u32[]{:S(2)}, u32[]{:S(2)}) async-start(bf16[8,1,32,4096]{3,2,1,0:T(8,128)(2,1)} %fusion), calls=%async_computation.4 | async-start | bytes 4194304 | tf_op jit(solution)/shard_map/all_to_all | solution.py:42
  170.6 21.9 %all-to-all-start.5 = ((bf16[32,2,2048]{2,1,0:T(2,128)(2,1)}), bf16[32,2,2048]{2,1,0:T(2,128)(2,1)S(1)}, u32[]{:S(2)}, u32[]{:S(2)}) async-start(bf16[32,2,2048]{2,1,0:T(2,128)(2,1)} %reshape.340), calls=%async_computation.5 | async-start | bytes 524288 | tf_op jit(solution)/shard_map/all_to_all | solution.py:192
where the time goes:
time: 199 us; the launch traced here: 197 us
  waiting for transfers between devices  81.4 us (41%)
  starting transfers between devices  40 us (20%)
  other arithmetic  26.7 us (13%)
  local copies, waits for them, and re-layouts  19.7 us (10%)
  blocking collectives  14.2 us (7%)
  matrix products  13.7 us (7%)
    all_to_all x4, waiting for transfers between devices, from_everyone(): return lax.all_to_all(copies, axis, split_axis=0, concat_axis=0, tiled=True)  45.9 us
    all_to_all x4, starting transfers between devices, from_everyone(): return lax.all_to_all(copies, axis, split_axis=0, concat_axis=0, tiled=True)  25.2 us
    all_to_all x1, waiting for transfers between devices, sent_and_summed(): lax.all_to_all(blocks, axis, split_axis=0, concat_axis=0, tiled=True)  23.8 us
    unnamed x2, other arithmetic  23.4 us
    all_to_all x1, blocking collectives, on_device(): lax.all_to_all(outgoing, 'expert', split_axis=0, concat_axis=2, tiled=True)  14.2 us
    all_to_all x1, waiting for transfers between devices, on_device(): lax.all_to_all(partial_out.astype(jnp.bfloat16), 'expert', split_axis=2,...  11.7 us
    all_to_all x1, starting transfers between devices, on_device(): lax.all_to_all(partial_out.astype(jnp.bfloat16), 'expert', split_axis=2,...  9.79 us
    dot_general x1, matrix products, on_device(): jnp.einsum('...f,fd->...d', hidden, expert_down[0], preferred_element_typ...  6.99 us
  transfers between devices with their start and end apart: 6, of which 5 were waited for; matrix products, arithmetic and copies ran while one was open for 8% of the time, Pallas kernels for 0%

commit v1 on v0

v1 whole, which is shorter than its diff:
```python
import jax
import jax.numpy as jnp
from jax import lax
from jax.experimental import pallas as pl
from jax.experimental.pallas import tpu as pltpu
from jax.sharding import PartitionSpec as P

D = 4096
E = 8
HD = 128
QH = 16
KVH = 4
STEPS = 2
ANSWERS = 128
EPSILON = 1e-05

ROWS = 64
PEERS = 32
LOCAL = 448
CHUNK = 1024
HALF = 512
SLOTS = 32
ORDER = (0, 1, 3, 2)

MESH = pl.DeviceIdType.MESH
F32 = jnp.float32
BF16 = jnp.bfloat16
NT = (((1,), (1,)), ((), ()))
NN = (((1,), (0,)), ((), ()))
NEG = -1e30


def dot(a, b, dims, precision=None):
    return lax.dot_general(a, b, dims, precision=precision, preferred_element_type=F32)


def iota(shape, dim):
    return lax.broadcasted_iota(jnp.int32, shape, dim)


def remote(src, dst, send_sem, recv_sem, device):
    return pltpu.make_async_remote_copy(
        src_ref=src,
        dst_ref=dst,
        send_sem=send_sem,
        recv_sem=recv_sem,
        device_id=device,
        device_id_type=MESH,
    )


def drain(ref, sem):
    pltpu.make_async_copy(ref, ref, sem).wait()


def layer(
    q_ref, nk_ref, nv_ref, len_ref, res_ref, gain_ref, router_ref, routes_ref, ans_ref, stop_ref,
    kc_ref, vc_ref, wo_hbm, wg_hbm, wu_hbm, wd_hbm,
    out_ref, share_ref,
    keys, values, wo, wg, wu, wd,
    qs, nks, nvs, att, attf, attm, stats, packed, disp, tok, gacc, uacc, hid,
    part, mate, zsum, hop_l, hop_r, fin, back, ret,
    load_sem, att_s, att_r, st_s, st_r, dp_s, dp_r,
    x_s, xl_r, xr_r, hl_r, hr_r, mt_r, y_s, my_r, yl_r, yr_r, fin_r, bk_s, bk_r,
):
    dp = lax.axis_index("dp")
    me = lax.axis_index("expert")
    x, c = lax.div(dp, 2), lax.rem(dp, 2)
    y, z = lax.div(me, 8), lax.rem(me, 8)
    xr, xl, xd = lax.rem(x + 1, 4), lax.rem(x + 3, 4), lax.rem(x + 2, 4)
    right, left, other = {"dp": xr * 2 + c}, {"dp": xl * 2 + c}, {"dp": x * 2 + 1 - c}
    expert = lax.div(me, 4)

    loads = [
        pltpu.make_async_copy(src, dst, load_sem.at[i])
        for i, (src, dst) in enumerate(
            (
                (kc_ref, keys),
                (vc_ref, values),
                (wo_hbm, wo),
                (wg_hbm, wg),
                (wu_hbm, wu),
                (wd_hbm, wd),
            )
        )
    ]
    for load in loads:
        load.start()

    barrier = pltpu.get_barrier_semaphore()

    def greet(i, carry):
        pl.semaphore_signal(
            barrier, inc=1, device_id={"expert": lax.rem(me + i, PEERS)}, device_id_type=MESH
        )
        return carry

    lax.fori_loop(1, PEERS, greet, 0)
    for neighbour in (right, left, other):
        pl.semaphore_signal(barrier, inc=1, device_id=neighbour, device_id_type=MESH)

    qf = q_ref[...].astype(F32)
    nkf = nk_ref[...].astype(F32)
    nvf = nv_ref[...].astype(F32)
    for kv in range(KVH):
        lanes = slice(kv * HD, (kv + 1) * HD)
        for t in range(STEPS):
            for g in range(4):
                h = kv * 4 + g
                r = kv * 8 + t * 4 + g
                qs[r : r + 1, :] = qf[t : t + 1, h * HD : (h + 1) * HD]
        for u in range(STEPS):
            nks[u, kv * 8 : kv * 8 + 8, :] = jnp.broadcast_to(nkf[u : u + 1, lanes], (8, HD))
            nvs[u, kv * 8 : kv * 8 + 8, :] = jnp.broadcast_to(nvf[u : u + 1, lanes], (8, HD))
    scale = HD ** (-0.5)
    qa = qs[...]
    qb = qa.astype(BF16)
    row = iota((32, 1), 0)
    second = lax.rem(lax.div(row, 4), 2) == 1
    fresh0 = jnp.sum(qa * nks[0], axis=1, keepdims=True) * scale
    fresh1 = jnp.sum(qa * nks[1], axis=1, keepdims=True) * scale
    fresh1 = jnp.where(second, fresh1, NEG)
    loads[0].wait()
    scores = jnp.concatenate(
        [
            dot(qb[kv * 8 : kv * 8 + 8], keys[:, kv * HD : (kv + 1) * HD], NT)
            for kv in range(KVH)
        ],
        axis=0,
    )
    scores = scores * scale
    scores = jnp.where(iota((32, 512), 1) < len_ref[0, 0], scores, NEG)
    top = jnp.maximum(jnp.maximum(jnp.max(scores, axis=1, keepdims=True), fresh0), fresh1)
    old = jnp.exp(scores - top)
    new0 = jnp.exp(fresh0 - top)
    new1 = jnp.exp(fresh1 - top)
    total = jnp.sum(old, axis=1, keepdims=True) + new0 + new1
    old = (old / total).astype(BF16)
    new0 = (new0 / total).astype(BF16).astype(F32)
    new1 = (new1 / total).astype(BF16).astype(F32)
    loads[1].wait()
    mixed_values = jnp.concatenate(
        [
            dot(old[kv * 8 : kv * 8 + 8], values[:, kv * HD : (kv + 1) * HD], NN)
            for kv in range(KVH)
        ],
        axis=0,
    )
    mixed_values = mixed_values + new0 * nvs[0] + new1 * nvs[1]
    att[me] = mixed_values.astype(BF16)

    pl.semaphore_wait(barrier, PEERS + 2)

    def send_att(i, carry):
        peer = lax.rem(me + i, PEERS)
        remote(att.at[me], att.at[me], att_s, att_r, {"expert": peer}).start()
        return carry

    lax.fori_loop(1, PEERS, send_att, 0)

    picks = jnp.concatenate([routes_ref[0, dp], routes_ref[1, dp]], axis=1)
    pick0, pick1 = picks[0:1, :], picks[1:2, :]
    names = iota((E, ROWS), 0)
    hot0, hot1 = (names == pick0).astype(F32), (names == pick1).astype(F32)
    a, b = iota((ROWS, ROWS), 0), iota((ROWS, ROWS), 1)
    before = ((a < b) & (lax.div(a, 32) == lax.div(b, 32))).astype(F32)
    earlier = dot((hot0 + hot1).astype(BF16), before.astype(BF16), NN)
    step_base = lax.div(iota((1, ROWS), 1), 32) * 16
    place0 = jnp.sum(earlier * hot0, axis=0, keepdims=True).astype(jnp.int32)
    place1 = jnp.sum(earlier * hot1, axis=0, keepdims=True).astype(jnp.int32)
    slot0 = pick0 * SLOTS + step_base + place0
    slot1 = pick1 * SLOTS + step_base + place1
    slots = iota((E * SLOTS, ROWS), 0)
    table = ((slots == slot0) | (slots == slot1)).astype(F32).astype(BF16)
    mine = iota((SLOTS, ROWS), 0) + expert * SLOTS
    own_table = ((mine == slot0) | (mine == slot1)).astype(F32)
    eye = a == b
    col0 = jnp.sum(jnp.where(eye, jnp.broadcast_to(slot0, (ROWS, ROWS)), 0), axis=1, keepdims=True)
    col1 = jnp.sum(jnp.where(eye, jnp.broadcast_to(slot1, (ROWS, ROWS)), 0), axis=1, keepdims=True)
    sign = hot0 - hot1
    sign_rows = dot(eye.astype(F32).astype(BF16), sign.astype(BF16), NT)

    hits = jnp.concatenate(
        [
            (iota((1, ANSWERS), 1) == ans_ref[0, t]).astype(F32)
            * (1 - stop_ref[0, t]).astype(F32)
            for t in range(STEPS)
        ],
        axis=0,
    )

    loads[2].wait()
    drain(att.at[0 : PEERS - 1], att_r)
    attf[...] = att[...].astype(F32).reshape(PEERS * 32, HD)
    for t in range(STEPS):
        for h in range(QH):
            r = (h // 4) * 8 + t * 4 + h % 4
            attm[t * 32 : (t + 1) * 32, h * HD : (h + 1) * HD] = attf[
                pl.ds(r, 32, stride=32), :
            ].astype(BF16)
    attn_proj = dot(attm[...], wo[...], NN)
    residual = res_ref[...].reshape(ROWS, HD).astype(F32)
    mixed = residual + attn_proj
    scaled = mixed * gain_ref[...].reshape(1, HD)
    squares = jnp.sum(mixed * mixed, axis=1, keepdims=True)
    logits = dot(scaled, router_ref[...], NT, lax.Precision.HIGHEST)
    apart = jnp.sum(logits * sign_rows, axis=1, keepdims=True)
    lane, line = iota((ROWS, 128), 1), iota((ROWS, 128), 0)
    line_up = jnp.where(lane == line, squares, jnp.where(lane == line + ROWS, apart, 0.0))
    stats[me, 0:1, :] = jnp.sum(line_up, axis=0, keepdims=True)
    stats[me, 1:3, :] = hits
    stats[me, 3:4, :] = jnp.zeros((1, 128), F32)

    def send_stats(i, carry):
        peer = lax.rem(me + i, PEERS)
        remote(stats.at[me], stats.at[me], st_s, st_r, {"expert": peer}).start()
        return carry

    lax.fori_loop(1, PEERS, send_stats, 0)

    packed[...] = dot(table, scaled.astype(BF16), NN).astype(BF16).reshape(E, SLOTS, HD)

    for dy in range(4):
        yd = lax.rem(y + dy, 4)

        def send_tokens(i, carry, dy=dy, yd=yd):
            peer = yd * 8 + lax.rem(z + i, 8)
            remote(
                packed.at[lax.div(peer, 4)],
                disp.at[me],
                dp_s,
                dp_r.at[(4 - dy) % 4],
                {"expert": peer},
            ).start()
            return carry

        lax.fori_loop(1 if dy == 0 else 0, 8, send_tokens, 0)
    disp[me] = packed[expert]

    cols = iota((ROWS, PEERS * SLOTS), 1)
    ids = lax.div(cols, 128) * SLOTS + lax.rem(cols, SLOTS)
    comb0 = (ids == col0).astype(F32).astype(BF16)
    comb1 = (ids == col1).astype(F32).astype(BF16)

    drain(stats.at[0 : PEERS - 1], st_r)
    sums = jnp.sum(stats[...], axis=0)
    squares_row, apart_row = sums[0:1, 0:ROWS], sums[0:1, ROWS:128]
    inv_row = lax.rsqrt(squares_row * (1.0 / D) + EPSILON)
    own_inv = jnp.sum(own_table * inv_row, axis=1, keepdims=True)
    gap_row = apart_row * inv_row
    gap = jnp.sum(jnp.where(eye, jnp.broadcast_to(gap_row, (ROWS, ROWS)), 0.0), axis=1, keepdims=True)
    tally0 = sums[1:2, :]
    tally1 = tally0 + sums[2:3, :]
    share_ref[0] = tally0 / jnp.maximum(jnp.sum(tally0, axis=1, keepdims=True), 1.0)
    share_ref[1] = tally1 / jnp.maximum(jnp.sum(tally1, axis=1, keepdims=True), 1.0)

    def block(xp, cp):
        return pl.ds(pl.multiple_of((cp * 4 + xp) * SLOTS, SLOTS), SLOTS)

    low, high = pl.ds(0, HALF), pl.ds(HALF, HALF)

    def spread_own(i):
        off = ORDER[i]
        qy = lax.rem(y + off, 4)
        drain(disp.at[0 : 7 if off == 0 else 8], dp_r.at[off])
        for k in range(8):
            rows = disp[qy * 8 + k].astype(F32) * own_inv
            tok[i, block(x, c), k * HD : (k + 1) * HD] = rows.astype(BF16)
        src = tok.at[i, block(x, c)]
        remote(src, src, x_s, xl_r.at[i], right).start()
        remote(src, src, x_s, xr_r.at[i], left).start()
        remote(src, src, x_s, mt_r.at[i], other).start()

    def spread_near(i):
        near = tok.at[i, block(xl, c)]
        drain(near, xl_r.at[i])
        half = tok.at[i, block(xl, c), low]
        remote(half, half, x_s, hl_r.at[i], right).start()
        remote(near, near, x_s, mt_r.at[i], other).start()
        near = tok.at[i, block(xr, c)]
        drain(near, xr_r.at[i])
        half = tok.at[i, block(xr, c), high]
        remote(half, half, x_s, hr_r.at[i], left).start()
        remote(near, near, x_s, mt_r.at[i], other).start()

    def spread_far(i):
        half = tok.at[i, block(xd, c), low]
        drain(half, hl_r.at[i])
        remote(half, half, x_s, mt_r.at[i], other).start()
        half = tok.at[i, block(xd, c), high]
        drain(half, hr_r.at[i])
        remote(half, half, x_s, mt_r.at[i], other).start()

    def multiply(i):
        qy = lax.rem(y + ORDER[i], 4)
        cut = pl.ds(pl.multiple_of(qy * CHUNK, CHUNK), CHUNK)
        drain(tok.at[i, pl.ds(0, 128)], mt_r.at[i])
        g = dot(tok[i], wg[:, cut], NT)
        u = dot(tok[i], wu[:, cut], NT)
        if i == 0:
            gacc[...] = g
            uacc[...] = u
        else:
            gacc[...] += g
            uacc[...] += u

    for step in range(4 + 3):
        if step < 4:
            spread_own(step)
        if 0 <= step - 1 < 4:
            spread_near(step - 1)
        if 0 <= step - 2 < 4:
            spread_far(step - 2)
        if step == 0:
            loads[3].wait()
            loads[4].wait()
        if 0 <= step - 3 < 4:
            multiply(step - 3)

    g = gacc[...]
    hid[...] = (g / (1.0 + jnp.exp(-g)) * uacc[...]).astype(BF16)
    loads[5].wait()

    def contribute(i):
        qy = lax.rem(y + ORDER[i], 4)
        cut = pl.ds(pl.multiple_of(qy * CHUNK, CHUNK), CHUNK)
        part[i] = dot(hid[...], wd[:, cut], NN).astype(BF16).reshape(2, 128, CHUNK)
        remote(part.at[i, 1 - c], mate.at[i], y_s, my_r.at[i], other).start()

    def pair_up(i):
        drain(mate.at[i], my_r.at[i])
        both = part[i, c].astype(F32) + mate[i].astype(F32)
        zsum[i] = both.astype(BF16).reshape(4, SLOTS, CHUNK)
        remote(zsum.at[i, xd, :, low], hop_l.at[i], y_s, yl_r.at[i], right).start()
        remote(zsum.at[i, xd, :, high], hop_r.at[i], y_s, yr_r.at[i], left).start()
        remote(zsum.at[i, xr, :, high], fin.at[i, 0], y_s, fin_r.at[i], right).start()
        remote(zsum.at[i, xl, :, low], fin.at[i, 2], y_s, fin_r.at[i], left).start()

    def pass_on(i):
        drain(hop_l.at[i], yl_r.at[i])
        zsum[i, xr, :, low] = (
            zsum[i, xr, :, low].astype(F32) + hop_l[i].astype(F32)
        ).astype(BF16)
        remote(zsum.at[i, xr, :, low], fin.at[i, 1], y_s, fin_r.at[i], right).start()
        drain(hop_r.at[i], yr_r.at[i])
        zsum[i, xl, :, high] = (
            zsum[i, xl, :, high].astype(F32) + hop_r[i].astype(F32)
        ).astype(BF16)
        remote(zsum.at[i, xl, :, high], fin.at[i, 3], y_s, fin_r.at[i], left).start()

    def give_back(i):
        qy = lax.rem(y + ORDER[i], 4)
        drain(fin.at[i], fin_r.at[i])
        for half in range(2):
            lanes = pl.ds(half * HALF, HALF)
            whole = (
                zsum[i, x, :, lanes].astype(F32)
                + fin[i, 1 - half].astype(F32)
                + fin[i, 2 + half].astype(F32)
            ).astype(BF16)
            for k in range(4):
                back[qy * 8 + half * 4 + k] = whole[:, k * HD : (k + 1) * HD]

        def send_back(k, carry):
            peer = qy * 8 + lax.rem(z + k, 8)
            remote(back.at[peer], ret.at[me], bk_s, bk_r, {"expert": peer}).start()
            return carry

        lax.fori_loop(1 if ORDER[i] == 0 else 0, 8, send_back, 0)

    for step in range(4 + 3):
        if step < 4:
            contribute(step)
        if 0 <= step - 1 < 4:
            pair_up(step - 1)
        if 0 <= step - 2 < 4:
            pass_on(step - 2)
        if 0 <= step - 3 < 4:
            give_back(step - 3)
    ret[me] = back[me]

    first_gate = 1.0 / (1.0 + jnp.exp(-gap))
    second_gate = 1.0 / (1.0 + jnp.exp(gap))
    drain(ret.at[0 : PEERS - 1], bk_r)
    arrived = ret[...].reshape(PEERS * SLOTS, HD)
    moe = first_gate * dot(comb0, arrived, NN) + second_gate * dot(comb1, arrived, NN)
    late = iota((ROWS, 1), 0) >= 32
    active = jnp.where(late, 1 - stop_ref[0, 1], 1 - stop_ref[0, 0]).astype(F32)
    updated = residual + active * (attn_proj + moe)
    out_ref[...] = updated.astype(BF16).reshape(STEPS, 1, 32, HD)

    drain(att.at[0 : PEERS - 1], att_s)
    drain(stats.at[0 : PEERS - 1], st_s)
    drain(disp.at[0 : PEERS - 1], dp_s)
    drain(tok.at[:, 0:224], x_s)
    drain(tok.at[:, 0:224], y_s)
    drain(ret.at[0 : PEERS - 1], bk_s)


def on_device(
    queries, cache_keys, cache_values, new_keys, new_values, cache_len, o_proj, residual_in,
    norm_gain, router, expert_gate, expert_up, expert_down, routes, answers, stop_mask,
):
    vmem = pl.BlockSpec(memory_space=pltpu.VMEM)
    smem = pl.BlockSpec(memory_space=pltpu.SMEM)
    anywhere = pl.BlockSpec(memory_space=pl.ANY)
    dma = pltpu.SemaphoreType.DMA
    return pl.pallas_call(
        layer,
        out_shape=(
            jax.ShapeDtypeStruct((STEPS, 1, 32, HD), BF16),
            jax.ShapeDtypeStruct((STEPS, 1, ANSWERS), F32),
        ),
        in_specs=[vmem] * 3 + [smem] + [vmem] * 4 + [smem] * 2 + [anywhere] * 6,
        out_specs=(vmem, vmem),
        scratch_shapes=[
            pltpu.VMEM((512, 512), BF16),
            pltpu.VMEM((512, 512), BF16),
            pltpu.VMEM((2048, HD), BF16),
            pltpu.VMEM((LOCAL, D), BF16),
            pltpu.VMEM((LOCAL, D), BF16),
            pltpu.VMEM((LOCAL, D), BF16),
            pltpu.VMEM((32, HD), F32),
            pltpu.VMEM((2, 32, HD), F32),
            pltpu.VMEM((2, 32, HD), F32),
            pltpu.VMEM((PEERS, 32, HD), BF16),
            pltpu.VMEM((PEERS * 32, HD), F32),
            pltpu.VMEM((ROWS, QH * HD), BF16),
            pltpu.VMEM((PEERS, 4, 128), F32),
            pltpu.VMEM((E, SLOTS, HD), BF16),
            pltpu.VMEM((PEERS, SLOTS, HD), BF16),
            pltpu.VMEM((4, 256, CHUNK), BF16),
            pltpu.VMEM((256, LOCAL), F32),
            pltpu.VMEM((256, LOCAL), F32),
            pltpu.VMEM((256, LOCAL), BF16),
            pltpu.VMEM((4, 2, 128, CHUNK), BF16),
            pltpu.VMEM((4, 128, CHUNK), BF16),
            pltpu.VMEM((4, 4, SLOTS, CHUNK), BF16),
            pltpu.VMEM((4, SLOTS, HALF), BF16),
            pltpu.VMEM((4, SLOTS, HALF), BF16),
            pltpu.VMEM((4, 4, SLOTS, HALF), BF16),
            pltpu.VMEM((PEERS, SLOTS, HD), BF16),
            pltpu.VMEM((PEERS, SLOTS, HD), BF16),
            dma((6,)),
            dma, dma, dma, dma, dma, dma((4,)),
            dma, dma((4,)), dma((4,)), dma((4,)), dma((4,)), dma((4,)),
            dma, dma((4,)), dma((4,)), dma((4,)), dma((4,)), dma, dma,
        ],
        compiler_params=pltpu.CompilerParams(collective_id=0, has_side_effects=True),
        name="decode_layer",
    )(
        queries.reshape(STEPS, QH * HD),
        new_keys.reshape(STEPS, KVH * HD),
        new_values.reshape(STEPS, KVH * HD),
        cache_len,
        residual_in,
        norm_gain,
        router.T,
        routes.transpose(0, 1, 3, 2),
        answers.reshape(1, STEPS),
        stop_mask.reshape(1, STEPS),
        cache_keys.reshape(512, 512),
        cache_values.reshape(512, 512),
        o_proj,
        expert_gate.transpose(0, 2, 1).reshape(LOCAL, D),
        expert_up.transpose(0, 2, 1).reshape(LOCAL, D),
        expert_down.reshape(LOCAL, D),
    )


def solution(mesh):
    placed = (
        P(None, "dp", "expert", None),
        P("dp", "expert", None, None),
        P("dp", "expert", None, None),
        P(None, "dp", "expert", None),
        P(None, "dp", "expert", None),
        P("dp", "expert"),
        P(None, "expert"),
        P(None, "dp", None, "expert"),
        P("expert"),
        P("expert", None),
        P("expert", None, "dp"),
        P("expert", None, "dp"),
        P("expert", "dp", None),
        P(),
        P(None, "dp", "expert"),
        P(None, "dp"),
    )
    return jax.shard_map(
        on_device,
        mesh=mesh,
        in_specs=placed,
        out_specs=(P(None, "dp", None, "expert"), P(None, "dp", None)),
        check_vma=False,
    )
```

time: 199 us -> 72.3 us (0.36)
  waiting for transfers between devices: 81.4 us -> 0 us
  Pallas kernels: 0 us -> 68.2 us
  starting transfers between devices: 40 us -> 0 us
  other arithmetic: 26.7 us -> 0 us
  local copies, waits for them, and re-layouts: 19.7 us -> 2.54 us
  blocking collectives: 14.2 us -> 0 us
  matrix products: 13.7 us -> 0 us
    all_to_all x6 -> x0, waiting for transfers between devices: 81.4 us -> none  [the longest x4 45.9 us: from_everyone(): return lax.all_to_all(copies, axis, split_axis=0, concat_axis=0, tiled=True)]
    pallas_call x0 -> x1, Pallas kernels: none -> 68.2 us  [on_device(): pl.pallas_call(layer, out_shape=(jax.ShapeDtypeStruct((STEPS, 1, 32, HD),...]
    all_to_all x6 -> x0, starting transfers between devices: 40 us -> none  [the longest x4 25.2 us: from_everyone(): return lax.all_to_all(copies, axis, split_axis=0, concat_axis=0, tiled=True)]
    unnamed x2 -> x0, other arithmetic: 23.4 us -> none
    all_to_all x1 -> x0, blocking collectives: 14.2 us -> none  [on_device(): lax.all_to_all(outgoing, 'expert', split_axis=0, concat_axis=2, tiled=True)]
    dot_general x11 -> x0, matrix products: 13.7 us -> none  [the longest x1 6.99 us: on_device(): jnp.einsum('...f,fd->...d', hidden, expert_down[0], preferred_element_typ...]
    broadcast_in_dim x5 -> x0, local copies, waits for them, and re-layouts: 3.75 us -> none  [the longest x4 3.71 us: from_everyone(): copies = jnp.broadcast_to(array, (lax.axis_size(axis), *array.shape))]
    another operation x4 -> x0, local copies, waits for them, and re-layouts: 3.11 us -> none
  transfers between devices with their start and end apart: 6 -> 0, of which waited for: 5 -> 0; matrix products, arithmetic and copies ran while one was open for 8% -> 0% of each run, Pallas kernels for 0% -> 0%
where the time goes in v1:
time: 72.3 us; the launch traced here: 72 us
  Pallas kernels  68.2 us (94%)
  local copies, waits for them, and re-layouts  2.54 us (4%)
  between operations  1.29 us (2%)
    pallas_call x1, Pallas kernels, on_device(): pl.pallas_call(layer, out_shape=(jax.ShapeDtypeStruct((STEPS, 1, 32, HD),...  68.2 us
    unnamed x2, local copies, waits for them, and re-layouts  2.54 us

profile of v1, /device:TPU:2, one launch (start us, length us, event | category | flops | bytes accessed | tf_op | source)
XLA Modules:
  0.0 72.0 jit_solution(9575274825402709945)
XLA Ops:
  1.3 68.2 %decode_layer.1 = (bf16[2,1,32,128]{3,2,1,0:T(8,128)(2,1)}, f32[2,1,128]{2,1,0:T(1,128)}) custom-call(bf16[2,2048]{1,0:T(2,128)(2,1)} %bitcast.22, bf16[2,512]{1,0:T(2,128)(2,1)} %bitcast.24, bf16[2,512]{1,0:T(2,128)(2,1)} %bitcast.25, s32[1,1]{1,0:T(1,128)S(6)} %copy.20.len_ref, bf16[2,1,32,128]{3,2,1,0:T(8,128)(2,1)} %res_ref.1, f32[128]{0:T(128)} %gain_ref.1, ...), custom_call_target="tpu_custom_call" | custom-call | tf_op jit(solution)/shard_map/decode_layer/pallas_call | solution.py:408
  69.5 1.3 %copy.21 = bf16[2,1,32,128]{3,2,1,0:T(8,128)(2,1)} copy(bf16[2,1,32,128]{3,2,1,0:T(8,128)(2,1)} %get-tuple-element.4) | data formatting | bytes 32768
  70.8 1.2 %copy.22 = f32[2,1,128]{2,1,0:T(1,128)} copy(f32[2,1,128]{2,1,0:T(1,128)} %get-tuple-element.5) | data formatting | bytes 2048

commit v2 on v1

v2 whole, which is shorter than its diff:
```python
import jax
import jax.numpy as jnp
from jax import lax
from jax.experimental import pallas as pl
from jax.experimental.pallas import tpu as pltpu
from jax.sharding import PartitionSpec as P

D = 4096
E = 8
HD = 128
QH = 16
KVH = 4
STEPS = 2
ANSWERS = 128
EPSILON = 1e-05

ROWS = 64
PEERS = 32
LOCAL = 448
CHUNK = 1024
HALF = 512
SLOTS = 32
ORDER = (0, 1, 3, 2)
BACK = (2, 1, 3, 0)
GATHER = (
    "own:0,own:1,near:0,own:2,sown:0,near:1,far:0,own:3,votes:0,near:2,far:1,near:3,snear:0,"
    "far:2,mul:0,far:3,sfar:0,mul:1,mul:2,mul:3"
)
RETURN = (
    "con:0,con:1,pair:0,con:2,pair:1,con:3,pair:2,pass:0,pair:3,pass:1,pass:2,give:0,"
    "pass:3,give:1,give:2,give:3"
)

MESH = pl.DeviceIdType.MESH
F32 = jnp.float32
BF16 = jnp.bfloat16
NT = (((1,), (1,)), ((), ()))
NN = (((1,), (0,)), ((), ()))
NEG = -1e30


def dot(a, b, dims, precision=None):
    return lax.dot_general(a, b, dims, precision=precision, preferred_element_type=F32)


def iota(shape, dim):
    return lax.broadcasted_iota(jnp.int32, shape, dim)


def remote(src, dst, send_sem, recv_sem, device):
    return pltpu.make_async_remote_copy(
        src_ref=src,
        dst_ref=dst,
        send_sem=send_sem,
        recv_sem=recv_sem,
        device_id=device,
        device_id_type=MESH,
    )


def drain(ref, sem):
    pltpu.make_async_copy(ref, ref, sem).wait()


def layer(
    q_hbm, nk_hbm, nv_hbm, len_hbm, res_hbm, gain_hbm, router_hbm, routes_hbm, ans_hbm, stop_hbm,
    kc_ref, vc_ref, wo_hbm, wg_hbm, wu_hbm, wd_hbm,
    out_ref, share_ref,
    q_ref, nk_ref, nv_ref, res_ref, gain_ref, router_ref, routes_ref, ans_ref, stop_ref,
    keys, values, wo, wg, wu, wd,
    qs, nks, nvs, att, attf, attm, stats, votes, packed, tok, invs, gacc, uacc, hid,
    part, mate, zsum, hop_l, hop_r, fin, back, ret,
    load_sem, att_s, att_r, st_s, st_r, vt_s, vt_r, dp_s, dp_r,
    x_s, xl_r, xr_r, hl_r, hr_r, mt_r, y_s, my_r, yl_r, yr_r, fin_r, bk_s, bk_r, in_s, in_r,
):
    dp = lax.axis_index("dp")
    me = lax.axis_index("expert")
    x, c = lax.div(dp, 2), lax.rem(dp, 2)
    y, z = lax.div(me, 8), lax.rem(me, 8)
    xr, xl, xd = lax.rem(x + 1, 4), lax.rem(x + 3, 4), lax.rem(x + 2, 4)
    right, left, other = {"dp": xr * 2 + c}, {"dp": xl * 2 + c}, {"dp": x * 2 + 1 - c}
    expert = lax.div(me, 4)

    def everyone(start):
        for dy in (2, 1, 3, 0):
            yd = lax.rem(y + dy, 4)

            def one(i, carry, dy=dy, yd=yd):
                half = lax.div(i + 1, 2)
                dz = jnp.where(lax.rem(i, 2) == 1, 4 - half, 4 + half)
                start(yd * 8 + lax.rem(z + dz, 8), dy)
                return carry

            lax.fori_loop(0, 7 if dy == 0 else 8, one, 0)

    with jax.named_scope("greet"):
        barrier = pltpu.get_barrier_semaphore()
        everyone(
            lambda peer, dy: pl.semaphore_signal(
                barrier, inc=1, device_id={"expert": peer}, device_id_type=MESH
            )
        )
        for neighbour in (right, left, other):
            pl.semaphore_signal(barrier, inc=1, device_id=neighbour, device_id_type=MESH)

        small = [
            (q_hbm, q_ref),
            (kc_ref, keys),
            (nk_hbm, nk_ref),
            (vc_ref, values),
            (nv_hbm, nv_ref),
            (routes_hbm, routes_ref),
            (ans_hbm, ans_ref),
            (stop_hbm, stop_ref),
            (res_hbm, res_ref),
            (gain_hbm, gain_ref),
            (router_hbm, router_ref),
            (wo_hbm, wo),
            (wg_hbm, wg),
            (wu_hbm, wu),
            (wd_hbm, wd),
        ]
        loads = [
            pltpu.make_async_copy(src, dst, load_sem.at[i]) for i, (src, dst) in enumerate(small)
        ]
        for load in loads:
            load.start()

    with jax.named_scope("attn"):
        for i in (0, 2, 4):
            loads[i].wait()
        qf = q_ref[...].astype(F32)
        nkf = nk_ref[...].astype(F32)
        nvf = nv_ref[...].astype(F32)
        for kv in range(KVH):
            lanes = slice(kv * HD, (kv + 1) * HD)
            for t in range(STEPS):
                for g in range(4):
                    h = kv * 4 + g
                    r = kv * 8 + t * 4 + g
                    qs[r : r + 1, :] = qf[t : t + 1, h * HD : (h + 1) * HD]
            for u in range(STEPS):
                nks[u, kv * 8 : kv * 8 + 8, :] = jnp.broadcast_to(nkf[u : u + 1, lanes], (8, HD))
                nvs[u, kv * 8 : kv * 8 + 8, :] = jnp.broadcast_to(nvf[u : u + 1, lanes], (8, HD))
        scale = HD ** (-0.5)
        qa = qs[...]
        qb = qa.astype(BF16)
        row = iota((32, 1), 0)
        second = lax.rem(lax.div(row, 4), 2) == 1
        fresh0 = jnp.sum(qa * nks[0], axis=1, keepdims=True) * scale
        fresh1 = jnp.sum(qa * nks[1], axis=1, keepdims=True) * scale
        fresh1 = jnp.where(second, fresh1, NEG)
        loads[1].wait()
        scores = jnp.concatenate(
            [
                dot(qb[kv * 8 : kv * 8 + 8], keys[:, kv * HD : (kv + 1) * HD], NT)
                for kv in range(KVH)
            ],
            axis=0,
        )
        scores = scores * scale
        scores = jnp.where(iota((32, 512), 1) < len_hbm[...], scores, NEG)
        top = jnp.maximum(jnp.maximum(jnp.max(scores, axis=1, keepdims=True), fresh0), fresh1)
        old = jnp.exp(scores - top)
        new0 = jnp.exp(fresh0 - top)
        new1 = jnp.exp(fresh1 - top)
        total = jnp.sum(old, axis=1, keepdims=True) + new0 + new1
        old = (old / total).astype(BF16)
        new0 = (new0 / total).astype(BF16).astype(F32)
        new1 = (new1 / total).astype(BF16).astype(F32)
        loads[3].wait()
        mixed_values = jnp.concatenate(
            [
                dot(old[kv * 8 : kv * 8 + 8], values[:, kv * HD : (kv + 1) * HD], NN)
                for kv in range(KVH)
            ],
            axis=0,
        )
        mixed_values = mixed_values + new0 * nvs[0] + new1 * nvs[1]
        att[me] = mixed_values.astype(BF16)

    with jax.named_scope("barrier"):
        pl.semaphore_wait(barrier, PEERS + 2)

    with jax.named_scope("sendatt"):
        everyone(
            lambda peer, dy: remote(
                att.at[me], att.at[me], att_s, att_r, {"expert": peer}
            ).start()
        )

    with jax.named_scope("slots"):
        for i in range(5, 12):
            loads[i].wait()
        picks = jnp.concatenate([routes_ref[0, dp], routes_ref[1, dp]], axis=1)
        pick0, pick1 = picks[0:1, :], picks[1:2, :]
        names = iota((E, ROWS), 0)
        hot0, hot1 = (names == pick0).astype(F32), (names == pick1).astype(F32)
        a, b = iota((ROWS, ROWS), 0), iota((ROWS, ROWS), 1)
        before = ((a < b) & (lax.div(a, 32) == lax.div(b, 32))).astype(F32)
        earlier = dot((hot0 + hot1).astype(BF16), before.astype(BF16), NN)
        step_base = lax.div(iota((1, ROWS), 1), 32) * 16
        place0 = jnp.sum(earlier * hot0, axis=0, keepdims=True).astype(jnp.int32)
        place1 = jnp.sum(earlier * hot1, axis=0, keepdims=True).astype(jnp.int32)
        slot0 = pick0 * SLOTS + step_base + place0
        slot1 = pick1 * SLOTS + step_base + place1
        slots = iota((E * SLOTS, ROWS), 0)
        table = ((slots == slot0) | (slots == slot1)).astype(F32).astype(BF16)
        eye = a == b
        sign = hot0 - hot1
        sign_rows = dot(eye.astype(F32).astype(BF16), sign.astype(BF16), NT)
        moving = 1 - stop_ref[...]
        lanes = iota((1, ANSWERS), 1)
        for t in range(STEPS):
            votes[me, t : t + 1, :] = (lanes == ans_ref[:, t : t + 1]).astype(F32) * moving[
                :, t : t + 1
            ].astype(F32)
        residual = res_ref[...].reshape(ROWS, HD).astype(F32)

    with jax.named_scope("waitatt"):
        drain(att.at[0 : PEERS - 1], att_r)
    with jax.named_scope("oproj"):
        attf[...] = att[...].astype(F32).reshape(PEERS * 32, HD)
        for t in range(STEPS):
            for h in range(QH):
                r = (h // 4) * 8 + t * 4 + h % 4
                attm[t * 32 : (t + 1) * 32, h * HD : (h + 1) * HD] = attf[
                    pl.ds(r, 32, stride=32), :
                ].astype(BF16)
        attn_proj = dot(attm[...], wo[...], NN)
        mixed = residual + attn_proj
        scaled = mixed * gain_ref[...].reshape(1, HD)
        packed[...] = dot(table, scaled.astype(BF16), NN).astype(BF16).reshape(E, SLOTS, HD)

    def block(xp, cp):
        return pl.ds(pl.multiple_of((cp * 4 + xp) * SLOTS, SLOTS), SLOTS)

    with jax.named_scope("sendtok"):
        for dy in ORDER:
            yd = lax.rem(y + dy, 4)

            def send_tokens(i, carry, dy=dy, yd=yd):
                peer = yd * 8 + lax.rem(z + i, 8)
                remote(
                    packed.at[lax.div(peer, 4)],
                    tok.at[ORDER.index((4 - dy) % 4), z, block(x, c)],
                    dp_s,
                    dp_r.at[ORDER.index((4 - dy) % 4)],
                    {"expert": peer},
                ).start()
                return carry

            lax.fori_loop(1 if dy == 0 else 0, 8, send_tokens, 0)
        tok[0, z, block(x, c)] = packed[expert]

    with jax.named_scope("stats"):
        squares = jnp.sum(mixed * mixed, axis=1, keepdims=True)
        logits = dot(scaled, router_ref[...], NT, lax.Precision.HIGHEST)
        apart = jnp.sum(logits * sign_rows, axis=1, keepdims=True)
        lane, line = iota((ROWS, 128), 1), iota((ROWS, 128), 0)
        line_up = jnp.where(lane == line, squares, jnp.where(lane == line + ROWS, apart, 0.0))
        stats[me] = jnp.sum(line_up, axis=0, keepdims=True)
        everyone(
            lambda peer, dy: remote(
                stats.at[me], stats.at[me], st_s, st_r, {"expert": peer}
            ).start()
        )

    with jax.named_scope("comb"):
        col0 = jnp.sum(
            jnp.where(eye, jnp.broadcast_to(slot0, (ROWS, ROWS)), 0), axis=1, keepdims=True
        )
        col1 = jnp.sum(
            jnp.where(eye, jnp.broadcast_to(slot1, (ROWS, ROWS)), 0), axis=1, keepdims=True
        )
        cols = iota((ROWS, PEERS * SLOTS), 1)
        ids = lax.div(cols, 128) * SLOTS + lax.rem(cols, SLOTS)
        comb0 = (ids == col0).astype(F32).astype(BF16)
        comb1 = (ids == col1).astype(F32).astype(BF16)

    low, high = pl.ds(0, HALF), pl.ds(HALF, HALF)
    first, last = pl.ds(0, 4), pl.ds(4, 4)

    def spread_own(i):
        src = tok.at[i, :, block(x, c)]
        drain(tok.at[i, pl.ds(0, 7 if i == 0 else 8), block(x, c)], dp_r.at[i])
        remote(src, src, x_s, xl_r.at[i], right).start()
        remote(src, src, x_s, xr_r.at[i], left).start()
        remote(src, src, x_s, mt_r.at[i], other).start()

    def spread_near(i):
        near = tok.at[i, :, block(xl, c)]
        drain(near, xl_r.at[i])
        half = tok.at[i, first, block(xl, c)]
        remote(half, half, x_s, hl_r.at[i], right).start()
        remote(near, near, x_s, mt_r.at[i], other).start()
        near = tok.at[i, :, block(xr, c)]
        drain(near, xr_r.at[i])
        half = tok.at[i, last, block(xr, c)]
        remote(half, half, x_s, hr_r.at[i], left).start()
        remote(near, near, x_s, mt_r.at[i], other).start()

    def spread_far(i):
        half = tok.at[i, first, block(xd, c)]
        drain(half, hl_r.at[i])
        remote(half, half, x_s, mt_r.at[i], other).start()
        half = tok.at[i, last, block(xd, c)]
        drain(half, hr_r.at[i])
        remote(half, half, x_s, mt_r.at[i], other).start()

    def multiply(i):
        qy = lax.rem(y + ORDER[i], 4)
        cut = pl.ds(pl.multiple_of(qy * CHUNK, CHUNK), CHUNK)
        drain(tok.at[i, :, pl.ds(0, 128)], mt_r.at[i])
        if i == 0:
            loads[12].wait()
            loads[13].wait()
        here = jnp.concatenate([tok[i, k] for k in range(8)], axis=1)
        g = dot(here, wg[:, cut], NT)
        u = dot(here, wu[:, cut], NT)
        if i == 0:
            gacc[...] = g
            uacc[...] = u
        else:
            gacc[...] += g
            uacc[...] += u

    def slot_of(xp, cp):
        return cp * 4 + xp

    def scales_own(i):
        drain(stats.at[0 : PEERS - 1], st_r)
        sums = jnp.sum(stats[...], axis=0)
        inv_row = lax.rsqrt(sums[:, 0:ROWS] * (1.0 / D) + EPSILON)
        gap_row = sums[:, ROWS:128] * inv_row
        mine = iota((SLOTS, ROWS), 0) + expert * SLOTS
        own_table = ((mine == slot0) | (mine == slot1)).astype(F32)
        own_inv = jnp.sum(own_table * inv_row, axis=1, keepdims=True)
        own_row = jnp.sum(
            jnp.where(iota((SLOTS, 128), 0) == iota((SLOTS, 128), 1), own_inv, 0.0),
            axis=0,
            keepdims=True,
        )
        invs[slot_of(x, c)] = own_row
        src = invs.at[slot_of(x, c)]
        remote(src, src, in_s, in_r.at[0], right).start()
        remote(src, src, in_s, in_r.at[1], left).start()
        remote(src, src, in_s, in_r.at[3], other).start()
        return jnp.sum(
            jnp.where(eye, jnp.broadcast_to(gap_row, (ROWS, ROWS)), 0.0), axis=1, keepdims=True
        )

    def scales_near(i):
        src = invs.at[slot_of(xl, c)]
        drain(src, in_r.at[0])
        remote(src, src, in_s, in_r.at[2], right).start()
        remote(src, src, in_s, in_r.at[3], other).start()
        src = invs.at[slot_of(xr, c)]
        drain(src, in_r.at[1])
        remote(src, src, in_s, in_r.at[3], other).start()

    def scales_far(i):
        src = invs.at[slot_of(xd, c)]
        drain(src, in_r.at[2])
        remote(src, src, in_s, in_r.at[3], other).start()

    def send_votes(i):
        everyone(
            lambda peer, dy: remote(
                votes.at[me], votes.at[me], vt_s, vt_r, {"expert": peer}
            ).start()
        )

    def contribute(i):
        qy = lax.rem(y + BACK[i], 4)
        cut = pl.ds(pl.multiple_of(qy * CHUNK, CHUNK), CHUNK)
        part[i] = dot(hid[...], wd[:, cut], NN).astype(BF16).reshape(2, 128, CHUNK)
        remote(part.at[i, 1 - c], mate.at[i], y_s, my_r.at[i], other).start()

    def pair_up(i):
        drain(mate.at[i], my_r.at[i])
        both = part[i, c].astype(F32) + mate[i].astype(F32)
        zsum[i] = both.astype(BF16).reshape(4, SLOTS, CHUNK)
        remote(zsum.at[i, xd, :, low], hop_l.at[i], y_s, yl_r.at[i], right).start()
        remote(zsum.at[i, xd, :, high], hop_r.at[i], y_s, yr_r.at[i], left).start()
        remote(zsum.at[i, xr, :, high], fin.at[i, 0], y_s, fin_r.at[i], right).start()
        remote(zsum.at[i, xl, :, low], fin.at[i, 2], y_s, fin_r.at[i], left).start()

    def pass_on(i):
        drain(hop_l.at[i], yl_r.at[i])
        zsum[i, xr, :, low] = (
            zsum[i, xr, :, low].astype(F32) + hop_l[i].astype(F32)
        ).astype(BF16)
        remote(zsum.at[i, xr, :, low], fin.at[i, 1], y_s, fin_r.at[i], right).start()
        drain(hop_r.at[i], yr_r.at[i])
        zsum[i, xl, :, high] = (
            zsum[i, xl, :, high].astype(F32) + hop_r[i].astype(F32)
        ).astype(BF16)
        remote(zsum.at[i, xl, :, high], fin.at[i, 3], y_s, fin_r.at[i], left).start()

    def give_back(i):
        qy = lax.rem(y + BACK[i], 4)
        drain(fin.at[i], fin_r.at[i])
        for half in range(2):
            lanes = pl.ds(half * HALF, HALF)
            whole = (
                zsum[i, x, :, lanes].astype(F32)
                + fin[i, 1 - half].astype(F32)
                + fin[i, 2 + half].astype(F32)
            ).astype(BF16)
            for k in range(4):
                back[qy * 8 + half * 4 + k] = whole[:, k * HD : (k + 1) * HD]

        def send_back(k, carry):
            half = lax.div(k + 1, 2)
            dz = jnp.where(lax.rem(k, 2) == 1, 4 - half, 4 + half)
            peer = qy * 8 + lax.rem(z + dz, 8)
            remote(back.at[peer], ret.at[me], bk_s, bk_r, {"expert": peer}).start()
            return carry

        lax.fori_loop(0, 7 if BACK[i] == 0 else 8, send_back, 0)

    named = {
        "own": spread_own, "near": spread_near, "far": spread_far, "mul": multiply,
        "sown": scales_own, "snear": scales_near, "sfar": scales_far, "votes": send_votes,
        "con": contribute, "pair": pair_up, "pass": pass_on, "give": give_back,
    }

    def run(plan):
        given = {}
        for word in plan.split(","):
            name, i = word.split(":")
            with jax.named_scope(name + i):
                given[name] = named[name](int(i))
        return given

    given = run(GATHER)
    gap = given["sown"]

    with jax.named_scope("hid"):
        drain(invs.at[0:4], in_r.at[3])
        column = jnp.concatenate(
            [
                jnp.sum(
                    jnp.where(iota((SLOTS, 128), 0) == iota((SLOTS, 128), 1), invs[n], 0.0),
                    axis=1,
                    keepdims=True,
                )
                for n in range(8)
            ],
            axis=0,
        )
        g = gacc[...] * column
        hid[...] = (g / (1.0 + jnp.exp(-g)) * (uacc[...] * column)).astype(BF16)
        loads[14].wait()

    run(RETURN)
    with jax.named_scope("gate"):
        ret[me] = back[me]
        first_gate = 1.0 / (1.0 + jnp.exp(-gap))
        second_gate = 1.0 / (1.0 + jnp.exp(gap))
        drain(votes.at[0 : PEERS - 1], vt_r)
        sums = jnp.sum(votes[...], axis=0)
        tally0 = sums[0:1, :]
        tally1 = tally0 + sums[1:2, :]
        share_ref[0] = tally0 / jnp.maximum(jnp.sum(tally0, axis=1, keepdims=True), 1.0)
        share_ref[1] = tally1 / jnp.maximum(jnp.sum(tally1, axis=1, keepdims=True), 1.0)
        late = iota((ROWS, 1), 0) >= 32
        active = jnp.where(late, moving[:, 1:2], moving[:, 0:1]).astype(F32)
    with jax.named_scope("waitret"):
        drain(ret.at[0 : PEERS - 1], bk_r)
    with jax.named_scope("final"):
        arrived = ret[...].reshape(PEERS * SLOTS, HD)
        moe = first_gate * dot(comb0, arrived, NN) + second_gate * dot(comb1, arrived, NN)
        updated = residual + active * (attn_proj + moe)
        out_ref[...] = updated.astype(BF16).reshape(STEPS, 1, 32, HD)

    with jax.named_scope("drain"):
        drain(att.at[0 : PEERS - 1], att_s)
        drain(stats.at[0 : PEERS - 1], st_s)
        drain(votes.at[0 : PEERS - 1], vt_s)
        drain(ret.at[0 : PEERS - 1], dp_s)
        drain(tok.at[:, :, 0:224], x_s)
        drain(tok.at[:, :, 0:224], y_s)
        drain(ret.at[0 : PEERS - 1], bk_s)
        drain(invs.at[0:7], in_s)


def on_device(
    queries, cache_keys, cache_values, new_keys, new_values, cache_len, o_proj, residual_in,
    norm_gain, router, expert_gate, expert_up, expert_down, routes, answers, stop_mask,
):
    vmem = pl.BlockSpec(memory_space=pltpu.VMEM)
    anywhere = pl.BlockSpec(memory_space=pltpu.HBM)
    dma = pltpu.SemaphoreType.DMA
    return pl.pallas_call(
        layer,
        out_shape=(
            pltpu.VMEM((STEPS, 1, 32, HD), BF16),
            pltpu.VMEM((STEPS, 1, ANSWERS), F32),
        ),
        in_specs=[anywhere] * 3 + [vmem] + [anywhere] * 12,
        out_specs=(vmem, vmem),
        scratch_shapes=[
            pltpu.VMEM((STEPS, QH * HD), BF16),
            pltpu.VMEM((STEPS, KVH * HD), BF16),
            pltpu.VMEM((STEPS, KVH * HD), BF16),
            pltpu.VMEM((STEPS, 1, 32, HD), BF16),
            pltpu.VMEM((HD,), F32),
            pltpu.VMEM((E, HD), F32),
            pltpu.VMEM((STEPS, 8, 2, 32), jnp.int32),
            pltpu.VMEM((1, STEPS), jnp.int32),
            pltpu.VMEM((1, STEPS), jnp.int32),
            pltpu.VMEM((512, 512), BF16),
            pltpu.VMEM((512, 512), BF16),
            pltpu.VMEM((2048, HD), BF16),
            pltpu.VMEM((LOCAL, D), BF16),
            pltpu.VMEM((LOCAL, D), BF16),
            pltpu.VMEM((LOCAL, D), BF16),
            pltpu.VMEM((32, HD), F32),
            pltpu.VMEM((2, 32, HD), F32),
            pltpu.VMEM((2, 32, HD), F32),
            pltpu.VMEM((PEERS, 32, HD), BF16),
            pltpu.VMEM((PEERS * 32, HD), F32),
            pltpu.VMEM((ROWS, QH * HD), BF16),
            pltpu.VMEM((PEERS, 1, 128), F32),
            pltpu.VMEM((PEERS, 2, 128), F32),
            pltpu.VMEM((E, SLOTS, HD), BF16),
            pltpu.VMEM((4, 8, 256, HD), BF16),
            pltpu.VMEM((8, 1, 128), F32),
            pltpu.VMEM((256, LOCAL), F32),
            pltpu.VMEM((256, LOCAL), F32),
            pltpu.VMEM((256, LOCAL), BF16),
            pltpu.VMEM((4, 2, 128, CHUNK), BF16),
            pltpu.VMEM((4, 128, CHUNK), BF16),
            pltpu.VMEM((4, 4, SLOTS, CHUNK), BF16),
            pltpu.VMEM((4, SLOTS, HALF), BF16),
            pltpu.VMEM((4, SLOTS, HALF), BF16),
            pltpu.VMEM((4, 4, SLOTS, HALF), BF16),
            pltpu.VMEM((PEERS, SLOTS, HD), BF16),
            pltpu.VMEM((PEERS, SLOTS, HD), BF16),
            dma((15,)),
            dma, dma, dma, dma, dma, dma, dma, dma((4,)),
            dma, dma((4,)), dma((4,)), dma((4,)), dma((4,)), dma((4,)),
            dma, dma((4,)), dma((4,)), dma((4,)), dma((4,)), dma, dma, dma, dma((4,)),
        ],
        compiler_params=pltpu.CompilerParams(collective_id=0, has_side_effects=True),
        name="decode_layer",
    )(
        queries.reshape(STEPS, QH * HD),
        new_keys.reshape(STEPS, KVH * HD),
        new_values.reshape(STEPS, KVH * HD),
        cache_len,
        residual_in,
        norm_gain,
        router.T,
        routes.transpose(0, 1, 3, 2),
        answers.reshape(1, STEPS),
        stop_mask.reshape(1, STEPS),
        cache_keys.reshape(512, 512),
        cache_values.reshape(512, 512),
        o_proj,
        expert_gate.transpose(0, 2, 1).reshape(LOCAL, D),
        expert_up.transpose(0, 2, 1).reshape(LOCAL, D),
        expert_down.reshape(LOCAL, D),
    )


def solution(mesh):
    placed = (
        P(None, "dp", "expert", None),
        P("dp", "expert", None, None),
        P("dp", "expert", None, None),
        P(None, "dp", "expert", None),
        P(None, "dp", "expert", None),
        P("dp", "expert"),
        P(None, "expert"),
        P(None, "dp", None, "expert"),
        P("expert"),
        P("expert", None),
        P("expert", None, "dp"),
        P("expert", None, "dp"),
        P("expert", "dp", None),
        P(),
        P(None, "dp", "expert"),
        P(None, "dp"),
    )
    return jax.shard_map(
        on_device,
        mesh=mesh,
        in_specs=placed,
        out_specs=(P(None, "dp", None, "expert"), P(None, "dp", None)),
        check_vma=False,
    )
```

time: 72.3 us -> 66 us (0.913)
  the two profiles are of different devices: /device:TPU:2 before, /device:TPU:1 now
where the time goes in v2:
time: 66 us; the launch traced here: 65.8 us
  Pallas kernels  63.4 us (96%)
  between operations  1.29 us (2%)
  local copies, waits for them, and re-layouts  1.17 us (2%)
    pallas_call x1, Pallas kernels, on_device(): pl.pallas_call(layer, out_shape=(pltpu.VMEM((STEPS, 1, 32, HD), BF16), pl...  63.4 us

profile of v2, /device:TPU:1, one launch (start us, length us, event | category | flops | bytes accessed | tf_op | source)
XLA Modules:
  0.0 65.8 jit_solution(9927357264644970706)
XLA Ops:
  1.3 63.4 %decode_layer.1 = (bf16[2,1,32,128]{3,2,1,0:T(8,128)(2,1)S(1)}, f32[2,1,128]{2,1,0:T(1,128)S(1)}) custom-call(bf16[2,2048]{1,0:T(2,128)(2,1)} %bitcast.22, bf16[2,512]{1,0:T(2,128)(2,1)} %bitcast.24, bf16[2,512]{1,0:T(2,128)(2,1)} %bitcast.25, s32[1,1]{1,0:T(1,128)S(6)} %copy.22.len_hbm, bf16[2,1,32,128]{3,2,1,0:T(8,128)(2,1)} %res_hbm.1, f32[128]{0:T(128)} %gain_hbm.1, ...), custom_call_target="tpu_custom_call" | custom-call | tf_op jit(solution)/shard_map/decode_layer/pallas_call | solution.py:496
  64.7 0.6 copy.20
  65.3 0.6 copy.21

commit v3 on v2

--- a/solution.py
+++ b/solution.py
@@ -20,14 +20,21 @@
 CHUNK = 1024
 HALF = 512
 SLOTS = 32
-ORDER = (0, 1, 3, 2)
-BACK = (2, 1, 3, 0)
+NEAREST = tuple(
+    sorted(
+        ((dy, dz) for dy in range(4) for dz in range(8)),
+        key=lambda o: (min(o[0], 4 - o[0]) + min(o[1], 8 - o[1]), o),
+    )
+)
+FARTHEST = NEAREST[::-1]
 GATHER = (
-    "own:0,own:1,near:0,own:2,sown:0,near:1,far:0,own:3,votes:0,near:2,far:1,near:3,snear:0,"
-    "far:2,mul:0,far:3,sfar:0,mul:1,mul:2,mul:3"
+    "own:0,own:1,own:2,near:0,own:3,near:1,sown:0,"
+    "near:2,far:0,near:3,far:1,snear:0,votes:0,far:2,"
+    "mul:0,far:3,sfar:0,mul:1,mul:2,column:0,mul:3"
 )
 RETURN = (
-    "con:0,con:1,pair:0,con:2,pair:1,con:3,pair:2,pass:0,pair:3,pass:1,pass:2,give:0,"
+    "con:0,con:1,pair:0,con:2,pair:1,con:3,"
+    "pass:0,pair:2,pass:1,pair:3,pass:2,give:0,"
     "pass:3,give:1,give:2,give:3"
 )
 
@@ -81,28 +88,19 @@
     right, left, other = {"dp": xr * 2 + c}, {"dp": xl * 2 + c}, {"dp": x * 2 + 1 - c}
     expert = lax.div(me, 4)
 
+    def at(dy, dz):
+        return lax.rem(y + dy, 4) * 8 + lax.rem(z + dz, 8)
+
+    def columns(ref, offsets):
+        return jnp.concatenate(
+            [ref[:, pl.ds(pl.multiple_of(at(*o) * HD, HD), HD)] for o in offsets], axis=1
+        )
+
     def everyone(start):
-        for dy in (2, 1, 3, 0):
-            yd = lax.rem(y + dy, 4)
-
-            def one(i, carry, dy=dy, yd=yd):
-                half = lax.div(i + 1, 2)
-                dz = jnp.where(lax.rem(i, 2) == 1, 4 - half, 4 + half)
-                start(yd * 8 + lax.rem(z + dz, 8), dy)
-                return carry
-
-            lax.fori_loop(0, 7 if dy == 0 else 8, one, 0)
+        for o in FARTHEST[:-1]:
+            start(at(*o))
 
     with jax.named_scope("greet"):
-        barrier = pltpu.get_barrier_semaphore()
-        everyone(
-            lambda peer, dy: pl.semaphore_signal(
-                barrier, inc=1, device_id={"expert": peer}, device_id_type=MESH
-            )
-        )
-        for neighbour in (right, left, other):
-            pl.semaphore_signal(barrier, inc=1, device_id=neighbour, device_id_type=MESH)
-
         small = [
             (q_hbm, q_ref),
             (kc_ref, keys),
@@ -125,6 +123,14 @@
         ]
         for load in loads:
             load.start()
+        barrier = pltpu.get_barrier_semaphore()
+        everyone(
+            lambda peer: pl.semaphore_signal(
+                barrier, inc=1, device_id={"expert": peer}, device_id_type=MESH
+            )
+        )
+        for neighbour in (right, left, other):
+            pl.semaphore_signal(barrier, inc=1, device_id=neighbour, device_id_type=MESH)
 
     with jax.named_scope("attn"):
         for i in (0, 2, 4):
@@ -184,7 +190,7 @@
 
     with jax.named_scope("sendatt"):
         everyone(
-            lambda peer, dy: remote(
+            lambda peer: remote(
                 att.at[me], att.at[me], att_s, att_r, {"expert": peer}
             ).start()
         )
@@ -236,22 +242,17 @@
         return pl.ds(pl.multiple_of((cp * 4 + xp) * SLOTS, SLOTS), SLOTS)
 
     with jax.named_scope("sendtok"):
-        for dy in ORDER:
-            yd = lax.rem(y + dy, 4)
-
-            def send_tokens(i, carry, dy=dy, yd=yd):
-                peer = yd * 8 + lax.rem(z + i, 8)
-                remote(
-                    packed.at[lax.div(peer, 4)],
-                    tok.at[ORDER.index((4 - dy) % 4), z, block(x, c)],
-                    dp_s,
-                    dp_r.at[ORDER.index((4 - dy) % 4)],
-                    {"expert": peer},
-                ).start()
-                return carry
-
-            lax.fori_loop(1 if dy == 0 else 0, 8, send_tokens, 0)
-        tok[0, z, block(x, c)] = packed[expert]
+        for dy, dz in NEAREST[1:]:
+            peer = at(dy, dz)
+            n = NEAREST.index(((4 - dy) % 4, (8 - dz) % 8))
+            remote(
+                packed.at[lax.div(peer, 4)],
+                tok.at[n // 8, n % 8, block(x, c)],
+                dp_s,
+                dp_r.at[n // 8],
+                {"expert": peer},
+            ).start()
+        tok[0, 0, block(x, c)] = packed[expert]
 
     with jax.named_scope("stats"):
         squares = jnp.sum(mixed * mixed, axis=1, keepdims=True)
@@ -261,7 +262,7 @@
         line_up = jnp.where(lane == line, squares, jnp.where(lane == line + ROWS, apart, 0.0))
         stats[me] = jnp.sum(line_up, axis=0, keepdims=True)
         everyone(
-            lambda peer, dy: remote(
+            lambda peer: remote(
                 stats.at[me], stats.at[me], st_s, st_r, {"expert": peer}
             ).start()
         )
@@ -309,15 +310,14 @@
         remote(half, half, x_s, mt_r.at[i], other).start()
 
     def multiply(i):
-        qy = lax.rem(y + ORDER[i], 4)
-        cut = pl.ds(pl.multiple_of(qy * CHUNK, CHUNK), CHUNK)
         drain(tok.at[i, :, pl.ds(0, 128)], mt_r.at[i])
         if i == 0:
             loads[12].wait()
             loads[13].wait()
         here = jnp.concatenate([tok[i, k] for k in range(8)], axis=1)
-        g = dot(here, wg[:, cut], NT)
-        u = dot(here, wu[:, cut], NT)
+        sources = NEAREST[i * 8 : i * 8 + 8]
+        g = dot(here, columns(wg, sources), NT)
+        u = dot(here, columns(wu, sources), NT)
         if i == 0:
             gacc[...] = g
             uacc[...] = u
@@ -364,17 +364,30 @@
         drain(src, in_r.at[2])
         remote(src, src, in_s, in_r.at[3], other).start()
 
+    def scale_column(i):
+        drain(invs.at[0:4], in_r.at[3])
+        return jnp.concatenate(
+            [
+                jnp.sum(
+                    jnp.where(iota((SLOTS, 128), 0) == iota((SLOTS, 128), 1), invs[n], 0.0),
+                    axis=1,
+                    keepdims=True,
+                )
+                for n in range(8)
+            ],
+            axis=0,
+        )
+
     def send_votes(i):
         everyone(
-            lambda peer, dy: remote(
+            lambda peer: remote(
                 votes.at[me], votes.at[me], vt_s, vt_r, {"expert": peer}
             ).start()
         )
 
     def contribute(i):
-        qy = lax.rem(y + BACK[i], 4)
-        cut = pl.ds(pl.multiple_of(qy * CHUNK, CHUNK), CHUNK)
-        part[i] = dot(hid[...], wd[:, cut], NN).astype(BF16).reshape(2, 128, CHUNK)
+        owners = FARTHEST[i * 8 : i * 8 + 8]
+        part[i] = dot(hid[...], columns(wd, owners), NN).astype(BF16).reshape(2, 128, CHUNK)
         remote(part.at[i, 1 - c], mate.at[i], y_s, my_r.at[i], other).start()
 
     def pair_up(i):
@@ -399,7 +412,6 @@
         remote(zsum.at[i, xl, :, high], fin.at[i, 3], y_s, fin_r.at[i], left).start()
 
     def give_back(i):
-        qy = lax.rem(y + BACK[i], 4)
         drain(fin.at[i], fin_r.at[i])
         for half in range(2):
             lanes = pl.ds(half * HALF, HALF)
@@ -409,20 +421,15 @@
                 + fin[i, 2 + half].astype(F32)
             ).astype(BF16)
             for k in range(4):
-                back[qy * 8 + half * 4 + k] = whole[:, k * HD : (k + 1) * HD]
-
-        def send_back(k, carry):
-            half = lax.div(k + 1, 2)
-            dz = jnp.where(lax.rem(k, 2) == 1, 4 - half, 4 + half)
-            peer = qy * 8 + lax.rem(z + dz, 8)
-            remote(back.at[peer], ret.at[me], bk_s, bk_r, {"expert": peer}).start()
-            return carry
-
-        lax.fori_loop(0, 7 if BACK[i] == 0 else 8, send_back, 0)
+                n = i * 8 + half * 4 + k
+                back[n] = whole[:, k * HD : (k + 1) * HD]
+                if n < PEERS - 1:
+                    peer = {"expert": at(*FARTHEST[n])}
+                    remote(back.at[n], ret.at[me], bk_s, bk_r, peer).start()
 
     named = {
         "own": spread_own, "near": spread_near, "far": spread_far, "mul": multiply,
-        "sown": scales_own, "snear": scales_near, "sfar": scales_far, "votes": send_votes,
+        "sown": scales_own, "snear": scales_near, "sfar": scales_far, "votes": send_votes, "column": scale_column,
         "con": contribute, "pair": pair_up, "pass": pass_on, "give": give_back,
     }
 
@@ -438,25 +445,14 @@
     gap = given["sown"]
 
     with jax.named_scope("hid"):
-        drain(invs.at[0:4], in_r.at[3])
-        column = jnp.concatenate(
-            [
-                jnp.sum(
-                    jnp.where(iota((SLOTS, 128), 0) == iota((SLOTS, 128), 1), invs[n], 0.0),
-                    axis=1,
-                    keepdims=True,
-                )
-                for n in range(8)
-            ],
-            axis=0,
-        )
+        column = given["column"]
         g = gacc[...] * column
         hid[...] = (g / (1.0 + jnp.exp(-g)) * (uacc[...] * column)).astype(BF16)
         loads[14].wait()
 
     run(RETURN)
     with jax.named_scope("gate"):
-        ret[me] = back[me]
+        ret[me] = back[PEERS - 1]
         first_gate = 1.0 / (1.0 + jnp.exp(-gap))
         second_gate = 1.0 / (1.0 + jnp.exp(gap))
         drain(votes.at[0 : PEERS - 1], vt_r)

time: 66 us -> 62.3 us (0.944)
  the two profiles are of different devices: /device:TPU:1 before, /device:TPU:2 now
where the time goes in v3:
time: 62.3 us; the launch traced here: 61.7 us
  Pallas kernels  59.2 us (95%)
  between operations  1.29 us (2%)
  local copies, waits for them, and re-layouts  1.17 us (2%)
    pallas_call x1, Pallas kernels, on_device(): pl.pallas_call(layer, out_shape=(pltpu.VMEM((STEPS, 1, 32, HD), BF16), pl...  59.2 us

profile of v3, /device:TPU:2, one launch (start us, length us, event | category | flops | bytes accessed | tf_op | source)
XLA Modules:
  0.0 61.7 jit_solution(15351060769354828376)
XLA Ops:
  1.3 59.2 %decode_layer.1 = (bf16[2,1,32,128]{3,2,1,0:T(8,128)(2,1)S(1)}, f32[2,1,128]{2,1,0:T(1,128)S(1)}) custom-call(bf16[2,2048]{1,0:T(2,128)(2,1)} %bitcast.22, bf16[2,512]{1,0:T(2,128)(2,1)} %bitcast.24, bf16[2,512]{1,0:T(2,128)(2,1)} %bitcast.25, s32[1,1]{1,0:T(1,128)S(6)} %copy.22.len_hbm, bf16[2,1,32,128]{3,2,1,0:T(8,128)(2,1)} %res_hbm.1, f32[128]{0:T(128)} %gain_hbm.1, ...), custom_call_target="tpu_custom_call" | custom-call | tf_op jit(solution)/shard_map/decode_layer/pallas_call | solution.py:492
  60.5 0.6 copy.20
  61.1 0.6 copy.21

commit v4 on v3

--- a/solution.py
+++ b/solution.py
@@ -27,15 +27,30 @@
     )
 )
 FARTHEST = NEAREST[::-1]
+OWNERS = tuple(
+    sorted(
+        range(PEERS),
+        key=lambda k: (k % 8 // 4, k % 8 // 4 * k // 8, k % 8 * 10 + (0, 12, 22, 23)[k // 8], k),
+    )
+)
 GATHER = (
-    "own:0,own:1,own:2,near:0,own:3,near:1,sown:0,"
-    "near:2,far:0,near:3,far:1,snear:0,votes:0,far:2,"
-    "mul:0,far:3,sfar:0,mul:1,mul:2,column:0,mul:3"
+    "own:0,own:1,own:2,near:0,own:3,near:1,sown:0"
+)
+GATHER_0 = (
+    "near:2,far:0,mul:0,near:3,far:1,snear:0,mul:1,far:2,"
+    "mul:2,far:3,sfar:0"
+)
+GATHER_1 = (
+    "near:2,far:0,near:3,far:1,snear:0,far:2,far:3,sfar:0,"
+    "mul:0,mul:1,mul:2"
+)
+GATHER_END = (
+    "column:0,mul:3"
 )
 RETURN = (
-    "con:0,con:1,pair:0,con:2,pair:1,con:3,"
-    "pass:0,pair:2,pass:1,pair:3,pass:2,give:0,"
-    "pass:3,give:1,give:2,give:3"
+    "con:0,con:1,pair:0,con:2,pair:1,con:3,votes:0,pass:0,"
+    "pair:2,pass:1,pair:3,pass:2,give:0,pass:3,give:1,give:2,"
+    "give:3"
 )
 
 MESH = pl.DeviceIdType.MESH
@@ -386,8 +401,9 @@
         )
 
     def contribute(i):
-        owners = FARTHEST[i * 8 : i * 8 + 8]
-        part[i] = dot(hid[...], columns(wd, owners), NN).astype(BF16).reshape(2, 128, CHUNK)
+        owners = OWNERS[i * 8 : i * 8 + 8]
+        wanted = jnp.concatenate([wd[:, k * HD : (k + 1) * HD] for k in owners], axis=1)
+        part[i] = dot(hid[...], wanted, NN).astype(BF16).reshape(2, 128, CHUNK)
         remote(part.at[i, 1 - c], mate.at[i], y_s, my_r.at[i], other).start()
 
     def pair_up(i):
@@ -410,6 +426,15 @@
             zsum[i, xl, :, high].astype(F32) + hop_r[i].astype(F32)
         ).astype(BF16)
         remote(zsum.at[i, xl, :, high], fin.at[i, 3], y_s, fin_r.at[i], left).start()
+
+    def send_back(n, owner):
+        @pl.when(me != owner)
+        def _():
+            remote(back.at[n], ret.at[me], bk_s, bk_r, {"expert": owner}).start()
+
+        @pl.when(me == owner)
+        def _():
+            ret[me] = back[n]
 
     def give_back(i):
         drain(fin.at[i], fin_r.at[i])
@@ -423,9 +448,7 @@
             for k in range(4):
                 n = i * 8 + half * 4 + k
                 back[n] = whole[:, k * HD : (k + 1) * HD]
-                if n < PEERS - 1:
-                    peer = {"expert": at(*FARTHEST[n])}
-                    remote(back.at[n], ret.at[me], bk_s, bk_r, peer).start()
+                send_back(n, OWNERS[n])
 
     named = {
         "own": spread_own, "near": spread_near, "far": spread_far, "mul": multiply,
@@ -441,8 +464,17 @@
                 given[name] = named[name](int(i))
         return given
 
-    given = run(GATHER)
-    gap = given["sown"]
+    gap = run(GATHER)["sown"]
+
+    @pl.when(c == 0)
+    def _():
+        run(GATHER_0)
+
+    @pl.when(c == 1)
+    def _():
+        run(GATHER_1)
+
+    given = run(GATHER_END)
 
     with jax.named_scope("hid"):
         column = given["column"]
@@ -452,7 +484,6 @@
 
     run(RETURN)
     with jax.named_scope("gate"):
-        ret[me] = back[PEERS - 1]
         first_gate = 1.0 / (1.0 + jnp.exp(-gap))
         second_gate = 1.0 / (1.0 + jnp.exp(gap))
         drain(votes.at[0 : PEERS - 1], vt_r)

time: 62.3 us -> 57.8 us (0.928)
  Pallas kernels: 59.2 us -> 55.2 us
    pallas_call x1, Pallas kernels: 59.2 us -> 55.2 us  [on_device(): pl.pallas_call(layer, out_shape=(pltpu.VMEM((STEPS, 1, 32, HD), BF16), pl...]
where the time goes in v4:
time: 57.8 us; the launch traced here: 57.7 us
  Pallas kernels  55.2 us (96%)
  between operations  1.29 us (2%)
  local copies, waits for them, and re-layouts  1.17 us (2%)
    pallas_call x1, Pallas kernels, on_device(): pl.pallas_call(layer, out_shape=(pltpu.VMEM((STEPS, 1, 32, HD), BF16), pl...  55.2 us
    unnamed x2, local copies, waits for them, and re-layouts  1.17 us

profile of v4, /device:TPU:2, one launch (start us, length us, event | category | flops | bytes accessed | tf_op | source)
XLA Modules:
  0.0 57.7 jit_solution(13245489677651642375)
XLA Ops:
  1.3 55.2 %decode_layer.1 = (bf16[2,1,32,128]{3,2,1,0:T(8,128)(2,1)S(1)}, f32[2,1,128]{2,1,0:T(1,128)S(1)}) custom-call(bf16[2,2048]{1,0:T(2,128)(2,1)} %bitcast.22, bf16[2,512]{1,0:T(2,128)(2,1)} %bitcast.24, bf16[2,512]{1,0:T(2,128)(2,1)} %bitcast.25, s32[1,1]{1,0:T(1,128)S(6)} %copy.22.len_hbm, bf16[2,1,32,128]{3,2,1,0:T(8,128)(2,1)} %res_hbm.1, f32[128]{0:T(128)} %gain_hbm.1, ...), custom_call_target="tpu_custom_call" | custom-call | tf_op jit(solution)/shard_map/decode_layer/pallas_call | solution.py:523
  56.5 0.6 %copy.20 = bf16[2,1,32,128]{3,2,1,0:T(8,128)(2,1)} copy(bf16[2,1,32,128]{3,2,1,0:T(8,128)(2,1)S(1)} %get-tuple-element.2) | data formatting | bytes 32768
  57.1 0.6 copy.21
